TPU v7x, 128 devices: a whole 4x4x4 slice. The times are simulated.
128 devices in a mesh: blk: 32 (over x, z, core), grp: 4 (over y).
Axes of the slice: x: 4, y: 4, z: 4, core: 2. Of those that a mesh axis runs over, the one named last changes fastest.
Arguments:
- statistics: float32 [4, 64, 512, 512], P('grp', 'blk'), as said below
- gradients: bfloat16 [4, 16, 512, 14336], P('grp', None, None, 'blk'), may hold values from -6 to 6
- live_counts: int32 [4, 32], P('grp'), may hold values from 0 to 2, as said below
- slot_row: int32 [4, 64], P('grp'), may hold values from 0 to 15, as said below
- sweeps: int32 [4, 64], P('grp', 'blk'), may hold values from 1 to 2, as said below
Outputs:
- updates: bfloat16 [4, 16, 512, 14336], P('grp', None, None, 'blk')
- off_max: float32 [2], replicated
Inputs may be any that keep to these rules, and one draw needn't show every extreme that they name: `live_counts`: the live slots of one index of grp number exactly 16; in every draw some device of each grp index has 2 live slots. `slot_row`: over the live slots of one index of grp each row block 0 to 15 appears exactly once. In each index of grp some live slot has 2 sweeps. `statistics`: every block is symmetric positive definite.
All inputs are finite; a program needn't handle non-finite values.
Results may differ from a plain program's by a relative error of at most 0.0051.
Values may be sent and summed in bfloat16 or wider, within the bound.
A program may use at most 192 MiB of HBM per device.

v0:
```python
import functools

import jax
import jax.numpy as jnp
from jax import lax
from jax.sharding import Mesh
from jax.sharding import PartitionSpec as P

MAXS = 2
BLK = ("blk_0", "blk_1", "blk_2")
BLK_GRP = ("blk_0", "blk_1", "blk_2", "grp")


damping = 0.01
pairings = ((0, 1, 2, 3), (0, 2, 1, 3), (0, 3, 1, 2))
highest = lax.Precision.HIGHEST


def by_axis(x, axes):
    return functools.reduce(lax.pmax, axes, x)


def regroup_cols(values, pairing, group_width):
    return jnp.concatenate(
        [values[:, member * group_width : (member + 1) * group_width] for member in pairing], axis=1
    )


def regroup(values, pairing, group_width):
    stacked = jnp.concatenate(
        [values[member * group_width : (member + 1) * group_width] for member in pairing], axis=0
    )
    return regroup_cols(stacked, pairing, group_width)


def angle_block(square_sub):
    group_width = square_sub.shape[-1] // 2
    diagonal = jnp.diagonal(square_sub, axis1=1, axis2=2)
    lower_diag = diagonal[:, :group_width, None]
    upper_diag = diagonal[:, None, group_width:]
    coupling = square_sub[:, :group_width, group_width:]
    difference = upper_diag - lower_diag
    bottom = (
        difference * difference
        + 4.0 * coupling * coupling
        + damping * (lower_diag + upper_diag) ** 2
    )
    return coupling * difference / bottom


def rotation_of(square_sub):
    angles = angle_block(square_sub)
    group_width = angles.shape[-1]
    identity = jnp.eye(group_width, dtype=jnp.float32)
    outer = jnp.einsum("hpq,hrq->hpr", angles, angles, precision=highest)
    inner = jnp.einsum("hqp,hqr->hpr", angles, angles, precision=highest)
    left_factor = jnp.linalg.cholesky(identity + 0.25 * outer)
    right_factor = jnp.linalg.cholesky(identity + 0.25 * inner)
    top_rows = jnp.concatenate([identity - 0.25 * outer, angles], axis=2)
    low_rows = jnp.concatenate([-jnp.swapaxes(angles, 1, 2), identity - 0.25 * inner], axis=2)
    top_half = jax.scipy.linalg.cho_solve((left_factor, True), top_rows)
    low_half = jax.scipy.linalg.cho_solve((right_factor, True), low_rows)
    return jnp.concatenate([top_half, low_half], axis=1)


def rotate_round(matrix, vectors, pairing):
    block_size = matrix.shape[0]
    group_width = block_size // 4
    restore = [pairing.index(member) for member in range(4)]
    matrix = regroup(matrix, pairing, group_width)
    vectors = regroup_cols(vectors, pairing, group_width)
    half_size = 2 * group_width
    square_sub = jnp.stack([matrix[:half_size, :half_size], matrix[half_size:, half_size:]])
    rotation = rotation_of(square_sub)
    row_part = jnp.einsum(
        "hpq,hpc->hqc", rotation, matrix.reshape(2, half_size, block_size), precision=highest
    )
    row_part = row_part.reshape(block_size, block_size)
    matrix = jnp.einsum(
        "rhp,hpq->rhq", row_part.reshape(block_size, 2, half_size), rotation, precision=highest
    )
    matrix = matrix.reshape(block_size, block_size)
    vectors = jnp.einsum(
        "rhp,hpq->rhq", vectors.reshape(block_size, 2, half_size), rotation, precision=highest
    )
    vectors = vectors.reshape(block_size, block_size)
    return (regroup(matrix, restore, group_width), regroup_cols(vectors, restore, group_width))


def one_sweep(matrix, vectors):
    for pairing in pairings:
        matrix, vectors = rotate_round(matrix, vectors, pairing)
    return (matrix, vectors)


def keep_both(matrix, vectors):
    return (matrix, vectors)


def off_norm(matrix):
    block_size = matrix.shape[0]
    on_diagonal = lax.broadcasted_iota(
        jnp.int32, (block_size, block_size), 0
    ) == lax.broadcasted_iota(jnp.int32, (block_size, block_size), 1)
    outside = jnp.where(on_diagonal, 0.0, matrix)
    return jnp.sqrt(jnp.sum(outside * outside) / jnp.sum(matrix * matrix))


def root_factor(matrix, vectors):
    scales = jnp.power(jnp.diagonal(matrix), -0.25)
    return jnp.dot(vectors * scales[None, :], vectors.T, precision=highest).astype(jnp.bfloat16)


def per_device(statistics, gradients, live_counts, slot_row, sweeps):
    matrices = statistics[0]
    slot_count = matrices.shape[0]
    block_size = matrices.shape[1]
    row_count = gradients.shape[1]
    blk_rank = lax.axis_index(BLK)
    own_live = lax.dynamic_index_in_dim(live_counts[0], blk_rank, 0, keepdims=False)
    own_sweeps = sweeps[0]
    identity = jnp.eye(block_size, dtype=jnp.float32)
    states = [matrices[slot_index] for slot_index in range(slot_count)]
    eigen_bases = [identity for slot_index in range(slot_count)]
    live_flags = [slot_index < own_live for slot_index in range(slot_count)]
    sweep_list = [own_sweeps[slot_index] for slot_index in range(slot_count)]
    local_peaks = jnp.zeros((MAXS,), jnp.float32)
    for slot_index in range(slot_count):
        for sweep_index in range(MAXS):
            active = jnp.logical_and(live_flags[slot_index], sweep_list[slot_index] > sweep_index)
            states[slot_index], eigen_bases[slot_index] = lax.cond(
                active, one_sweep, keep_both, states[slot_index], eigen_bases[slot_index]
            )
            local_peaks = local_peaks.at[sweep_index].max(
                jnp.where(active, off_norm(states[slot_index]), jnp.float32(0.0))
            )
    off_max = by_axis(local_peaks, BLK_GRP)
    blank_factor = jnp.zeros((block_size, block_size), jnp.bfloat16)
    factor_list = [
        jnp.where(
            live_flags[slot_index],
            root_factor(states[slot_index], eigen_bases[slot_index]),
            blank_factor,
        )
        for slot_index in range(slot_count)
    ]
    factors = jnp.stack(factor_list)
    row_ids = lax.iota(jnp.int32, row_count)
    gathered = lax.all_gather(factors, BLK, axis=0, tiled=True)
    slot_total = gathered.shape[0]
    slot_ids = lax.iota(jnp.int32, slot_total)
    is_live = slot_ids % slot_count < jnp.repeat(live_counts[0], slot_count)
    matches = (slot_row[0][None, :] == row_ids[:, None]) & is_live[None, :]
    slot_of = jnp.sum(jnp.where(matches, slot_ids[None, :], 0), axis=1)
    chosen = jnp.take(gathered, slot_of, axis=0)
    updates = jnp.einsum("kij,kjc->kic", chosen, gradients[0], preferred_element_type=jnp.float32)
    return (updates.astype(jnp.bfloat16)[None], off_max)


def solution(mesh):
    split = Mesh(
        mesh.devices.reshape(4, 4, 2, mesh.shape["grp"]), ("blk_0", "blk_1", "blk_2", "grp")
    )
    return jax.shard_map(
        per_device,
        mesh=split,
        in_specs=(
            P("grp", BLK, None, None),
            P("grp", None, None, BLK),
            P("grp", None),
            P("grp", None),
            P("grp", BLK),
        ),
        out_specs=(P("grp", None, None, BLK), P()),
        check_vma=False,
    )
```

profile of v0, /device:TPU:1, one launch (start us, length us, event | category | flops | bytes accessed | tf_op | source)
XLA Modules:
  0.0 1782.6 jit_solution(11419021902682509797)
XLA Ops:
  17.2 372.8 %conditional.4 = (f32[512,512]{0,1:T(8,128)S(1)}, f32[512,512]{0,1:T(8,128)S(1)}) conditional(s32[]{:T(128)} %convert_element_type.155, (f32[512,512]{1,0:T(8,128)S(1)}, f32[512,512]{0,1:T(8,128)S(1)}) %tuple.70, (f32[512,512]{1,0:T(8,128)S(1)}, f32[512,512]{0,1:T(8,128)S(1)}) %tuple.70), branch_computations={%region_1.2_spmd, %region_2.7_spmd} | conditional | flops 8781105152 | bytes 108000352 | solution.py:131
  18.2 17.2 copy.767
  38.6 23.5 %custom-call.84 = f32[2,128,128]{2,1,0:T(8,128)S(1)} custom-call(f32[2,128,128]{2,1,0:T(8,128)S(1)} %fusion.75), custom_call_target="Cholesky" | custom-call | tf_op jit(solution)/shard_map/cond/branch_1_fun/jit(cholesky)/cholesky | solution.py:58
  62.6 23.5 %custom-call.82 = f32[2,128,128]{2,1,0:T(8,128)S(1)} custom-call(f32[2,128,128]{2,1,0:T(8,128)S(1)} %copy.773), custom_call_target="Cholesky" | custom-call | tf_op jit(solution)/shard_map/cond/branch_1_fun/jit(cholesky)/cholesky | solution.py:57
  87.0 20.1 %custom-call.83 = f32[2,1,128,128]{2,3,1,0:T(8,128)S(1)} custom-call(f32[2,1,128,128]{3,2,1,0:T(8,128)S(1)} %get-tuple-element.295), custom_call_target="InvertDiagBlocksLowerTriangular" | custom-call | tf_op jit(solution)/shard_map/cond/branch_1_fun/jit(_cho_solve)/vmap()/triangular_solve | solution.py:61
  108.0 20.5 %custom-call.85 = f32[2,1,128,128]{2,3,1,0:T(8,128)S(1)} custom-call(f32[2,1,128,128]{3,2,1,0:T(8,128)} %get-tuple-element.296), custom_call_target="InvertDiagBlocksLowerTriangular" | custom-call | tf_op jit(solution)/shard_map/cond/branch_1_fun/jit(_cho_solve)/vmap()/triangular_solve | solution.py:62
  142.2 16.6 copy.788
  163.4 23.5 %custom-call.86 = f32[2,128,128]{2,1,0:T(8,128)S(1)} custom-call(f32[2,128,128]{2,1,0:T(8,128)S(1)} %fusion.71), custom_call_target="Cholesky" | custom-call | tf_op jit(solution)/shard_map/cond/branch_1_fun/jit(cholesky)/cholesky | solution.py:57
  187.0 23.5 %custom-call.88 = f32[2,128,128]{2,1,0:T(8,128)S(1)} custom-call(f32[2,128,128]{2,1,0:T(8,128)S(1)} %fusion.67), custom_call_target="Cholesky" | custom-call | tf_op jit(solution)/shard_map/cond/branch_1_fun/jit(cholesky)/cholesky | solution.py:58
  210.9 19.9 %custom-call.87 = f32[2,1,128,128]{2,3,1,0:T(8,128)S(1)} custom-call(f32[2,1,128,128]{3,2,1,0:T(8,128)S(1)} %get-tuple-element.293), custom_call_target="InvertDiagBlocksLowerTriangular" | custom-call | tf_op jit(solution)/shard_map/cond/branch_1_fun/jit(_cho_solve)/vmap()/triangular_solve | solution.py:61
  231.6 19.7 %custom-call.89 = f32[2,1,128,128]{2,3,1,0:T(8,128)S(1)} custom-call(f32[2,1,128,128]{3,2,1,0:T(8,128)S(1)} %get-tuple-element.294), custom_call_target="InvertDiagBlocksLowerTriangular" | custom-call | tf_op jit(solution)/shard_map/cond/branch_1_fun/jit(_cho_solve)/vmap()/triangular_solve | solution.py:62
  267.4 16.5 copy.812
  287.0 23.9 %custom-call.92 = f32[2,128,128]{2,1,0:T(8,128)S(1)} custom-call(f32[2,128,128]{2,1,0:T(8,128)S(1)} %fusion.59), custom_call_target="Cholesky" | custom-call | tf_op jit(solution)/shard_map/cond/branch_1_fun/jit(cholesky)/cholesky | solution.py:58
  311.5 23.5 %custom-call.90 = f32[2,128,128]{2,1,0:T(8,128)S(1)} custom-call(f32[2,128,128]{2,1,0:T(8,128)S(1)} %copy.818), custom_call_target="Cholesky" | custom-call | tf_op jit(solution)/shard_map/cond/branch_1_fun/jit(cholesky)/cholesky | solution.py:57
  336.8 19.7 %custom-call.91 = f32[2,1,128,128]{2,3,1,0:T(8,128)S(1)} custom-call(f32[2,1,128,128]{3,2,1,0:T(8,128)S(1)} %get-tuple-element.291), custom_call_target="InvertDiagBlocksLowerTriangular" | custom-call | tf_op jit(solution)/shard_map/cond/branch_1_fun/jit(_cho_solve)/vmap()/triangular_solve | solution.py:61
  357.3 19.8 %custom-call.93 = f32[2,1,128,128]{2,3,1,0:T(8,128)S(1)} custom-call(f32[2,1,128,128]{3,2,1,0:T(8,128)S(1)} %get-tuple-element.292), custom_call_target="InvertDiagBlocksLowerTriangular" | custom-call | tf_op jit(solution)/shard_map/cond/branch_1_fun/jit(_cho_solve)/vmap()/triangular_solve | solution.py:62
  392.6 15.4 conditional.5
  407.9 8.9 gather_fusion.12
  416.9 10.5 conditional.6
  431.3 11.1 conditional.7
  470.0 1194.3 %pmax.28 = f32[2]{0:T(128)S(1)} all-reduce(f32[2]{0:T(128)S(1)} %maximum_dynamic-update-slice_fusion), channel_id=1, replica_groups=mesh['blk_0'=4,'blk_1'=4,'blk_2'=2,'grp'=4] {'blk_0'}, use_global_device_ids=true, to_apply=%region_19.22 | all-reduce | flops 2 | bytes 16 | tf_op jit(solution)/shard_map/pmax | solution.py:20
  1673.7 14.5 pmax.31
  1689.3 69.4 %all-gather.2.cloned.1.call-done = bf16[64,512,512]{2,1,0:T(8,128)(2,1)} async-done(((bf16[2,512,512]{2,1,0:T(8,128)(2,1)}), bf16[64,512,512]{2,1,0:T(8,128)(2,1)}) %all-gather.2.cloned.1.call-update) | async-done | bytes 33554448 | tf_op jit(solution)/shard_map/all_gather | solution.py:149
  1764.9 10.6 convert_bitcast_fusion
  (161 shorter events, 117.1 us)
Async XLA Ops:
  7.2 1751.5 %all-gather.2.cloned.1.call-start = ((), (), s32[]{:S(2)}) async-start(), calls=%async_computation | async-start | bytes 34603008 | tf_op jit(solution)/shard_map/all_gather | solution.py:149
  17.2 193.3 %copy-start.17 = (pred[128,128]{1,0:T(8,128)(4,1)}, pred[128,128]{1,0:T(8,128)(4,1)S(1)}, u32[]{:S(2)}) copy-start(pred[128,128]{1,0:T(8,128)(4,1)S(1)} %iota_compare_fusion.7) | copy-start | bytes 49156 | tf_op jit(solution)/shard_map/cond
  17.2 193.5 %copy-start.13 = (pred[128,128]{1,0:T(8,128)(4,1)}, pred[128,128]{1,0:T(8,128)(4,1)S(1)}, u32[]{:S(2)}) copy-start(pred[128,128]{1,0:T(8,128)(4,1)S(1)} %iota_compare_fusion.6) | copy-start | bytes 49156 | tf_op jit(solution)/shard_map/cond
  431.3 1257.0 %copy-start.21 = (s32[1,32]{1,0:T(1,128)S(1)}, s32[1,32]{1,0:T(1,128)}, u32[]{:S(2)}) copy-start(s32[1,32]{1,0:T(1,128)} %param.26) | copy-start | bytes 388
Sparse Core Ops, SparseCore 0:
  456.7 1301.9 all-gather.1
where the time goes:
time: 1800 us; the launch traced here: 1780 us
  blocking collectives  1220 us (68%)
  other arithmetic  282 us (16%)
  local copies, waits for them, and re-layouts  112 us (6%)
  waiting for transfers between devices  69.4 us (4%)
  matrix products  44 us (2%)
  loops' own time  32.1 us (2%)
  between operations  24.6 us (1%)
    pmax x4, blocking collectives, by_axis(): return functools.reduce(lax.pmax, axes, x)  1220 us
    another operation x9, other arithmetic, rotation_of(): left_factor = jnp.linalg.cholesky(identity + 0.25 * outer)  71.5 us
    another operation x6, other arithmetic, rotation_of(): right_factor = jnp.linalg.cholesky(identity + 0.25 * inner)  71.2 us
    all_gather x1, waiting for transfers between devices, per_device(): gathered = lax.all_gather(factors, BLK, axis=0, tiled=True)  69.4 us
    another operation x7, other arithmetic, rotation_of(): top_half = jax.scipy.linalg.cho_solve((left_factor, True), top_rows)  61.4 us
    another operation x3, other arithmetic, rotation_of(): low_half = jax.scipy.linalg.cho_solve((right_factor, True), low_rows)  60 us
    another operation x4, local copies, waits for them, and re-layouts, rotate_round(): jnp.stack([matrix[:half_size, :half_size], matrix[half_size:, half_size:]])  50.3 us
  transfers between devices with their start and end apart: 1, of which 1 were waited for; matrix products, arithmetic and copies ran while one was open for 0% of the time, Pallas kernels for 0%

commit v1 on v0

v1 whole, which is shorter than its diff:
```python
import functools
import jax
import jax.numpy as jnp
from jax import lax
from jax.experimental import pallas as pl
from jax.experimental.pallas import tpu as pltpu
from jax.sharding import Mesh
from jax.sharding import PartitionSpec as P

MAXS = 2
GW = 128
damping = 0.01
pairings = ((0, 1, 2, 3), (0, 2, 1, 3), (0, 3, 1, 2))
f32, bf16 = jnp.float32, jnp.bfloat16
TOL = 1e-6
DOUBLINGS = 4


def split(x):
    hi = x.astype(bf16)
    return hi, (x - hi.astype(f32)).astype(bf16)


def dot3(a, b):
    dot = functools.partial(jnp.dot, preferred_element_type=f32)
    return dot(a[0], b[0]) + (dot(a[1], b[0]) + dot(a[0], b[1]))


def grp(member):
    return slice(member * GW, (member + 1) * GW)


def eye_mask(size):
    rows = lax.broadcasted_iota(jnp.int32, (size, size), 0)
    return rows == lax.broadcasted_iota(jnp.int32, (size, size), 1)


def sweep_body(slots, m_ref, v_ref, y_ref, t_ref, p_ref):
    mask = eye_mask(GW)
    identity = mask.astype(f32)
    for pairing in pairings:
        jobs = [(s, pairing[2 * h], pairing[2 * h + 1]) for s in slots for h in range(2)]
        angles, alphas = [], []
        peak = None
        for j, (s, a, b) in enumerate(jobs):
            low = jnp.sum(jnp.where(mask, m_ref[s, grp(a), grp(a)], 0.0), axis=1, keepdims=True)
            up = jnp.sum(jnp.where(mask, m_ref[s, grp(b), grp(b)], 0.0), axis=0, keepdims=True)
            c = m_ref[s, grp(a), grp(b)]
            diff = up - low
            both = up + low
            ang = c * diff / (diff * diff + 4.0 * c * c + damping * (both * both))
            ang_t = ang.T
            sa, sat = split(ang), split(ang_t)
            bb = 0.25 * dot3(sa, sat)
            bound = jnp.max(jnp.sum(jnp.abs(bb), axis=0, keepdims=True), axis=1, keepdims=True)
            alpha = 2.0 / (2.0 + bound)
            cc = (1.0 - alpha) * identity - alpha * bb
            sc = split(cc)
            t = identity + cc
            p = dot3(sc, sc)
            for k in range(1, DOUBLINGS):
                sp = split(p)
                t = t + dot3(split(t), sp)
                if k < DOUBLINGS - 1:
                    p = dot3(sp, sp)
            t_ref[j] = t
            p_ref[j] = p
            angles.append((ang, sa, sat))
            alphas.append(alpha)
            peak = bound if peak is None else jnp.maximum(peak, bound)
        rho = jnp.max(peak / (2.0 + peak))
        for _ in range(DOUBLINGS):
            rho = rho * rho

        def more(r):
            for j in range(len(jobs)):
                sp = split(p_ref[j])
                p = dot3(sp, sp)
                p_ref[j] = p
                t = t_ref[j]
                t_ref[j] = t + dot3(split(t), split(p))
            return r * r

        lax.while_loop(lambda r: r > TOL, more, rho)

        rots = []
        for j in range(len(jobs)):
            ang, sa, sat = angles[j]
            w = alphas[j] * t_ref[j]
            x = dot3(split(w), sa)
            q = identity - 0.5 * dot3(sat, split(x))
            p = 2.0 * w - identity
            xt = x.T
            r = jnp.concatenate(
                [jnp.concatenate([p, x], axis=1), jnp.concatenate([-xt, q], axis=1)], axis=0
            )
            rt = jnp.concatenate(
                [jnp.concatenate([p, -x], axis=1), jnp.concatenate([xt, q], axis=1)], axis=0
            )
            rots.append((split(r), split(rt)))
        for j, (s, a, b) in enumerate(jobs):
            cols = jnp.concatenate([m_ref[s, :, grp(a)], m_ref[s, :, grp(b)]], axis=1)
            y = dot3(split(cols), rots[j][0])
            y_ref[s, :, grp(a)] = y[:, :GW]
            y_ref[s, :, grp(b)] = y[:, GW:]
        for j, (s, a, b) in enumerate(jobs):
            rows = jnp.concatenate([y_ref[s, grp(a), :], y_ref[s, grp(b), :]], axis=0)
            z = dot3(rots[j][1], split(rows))
            m_ref[s, grp(a), :] = z[:GW]
            m_ref[s, grp(b), :] = z[GW:]
        for j, (s, a, b) in enumerate(jobs):
            cols = jnp.concatenate([v_ref[s, :, grp(a)], v_ref[s, :, grp(b)]], axis=1)
            y = dot3(split(cols), rots[j][0])
            v_ref[s, :, grp(a)] = y[:, :GW]
            v_ref[s, :, grp(b)] = y[:, GW:]


def off_norm(matrix, mask):
    square = matrix * matrix
    off = jnp.sum(jnp.where(mask, 0.0, square))
    return jnp.sqrt(off / jnp.sum(square))


def finish(slots, m_ref, v_ref, f_ref, mask):
    for s in slots:
        diagonal = jnp.sum(jnp.where(mask, m_ref[s], 0.0), axis=0, keepdims=True)
        eighth = jnp.sqrt(lax.rsqrt(jnp.sqrt(diagonal)))
        hi, lo = split(v_ref[s] * eighth)
        dot = functools.partial(
            lax.dot_general, dimension_numbers=(((1,), (1,)), ((), ())), preferred_element_type=f32
        )
        f_ref[s] = (dot(hi, hi) + (dot(lo, hi) + dot(hi, lo))).astype(bf16)


def jacobi_kernel(counts_ref, stats_ref, f_ref, off_ref, m_ref, v_ref, y_ref, t_ref, p_ref):
    size = stats_ref.shape[1]
    mask = eye_mask(size)
    n0, n1 = counts_ref[0], counts_ref[1]
    for i in range(MAXS):
        for s in range(2):
            off_ref[i, s] = 0.0
    scratch = (m_ref, v_ref, y_ref, t_ref, p_ref)

    @pl.when(n0 > 0)
    def _():
        m_ref[...] = stats_ref[...]
        for s in range(2):
            v_ref[s] = mask.astype(f32)

    def sweep(i, carry):
        a0, a1 = n0 > i, n1 > i
        slot = jnp.where(a0, 0, 1)

        @pl.when(a0 & a1)
        def _():
            sweep_body((0, 1), *scratch)
            off_ref[i, 0] = off_norm(m_ref[0], eye_mask(size))
            off_ref[i, 1] = off_norm(m_ref[1], eye_mask(size))

        @pl.when(a0 != a1)
        def _():
            sweep_body((slot,), *scratch)
            off_ref[i, slot] = off_norm(m_ref[slot], eye_mask(size))

        return carry

    lax.fori_loop(0, MAXS, sweep, 0)

    @pl.when(n0 > 0)
    def _():
        finish((0,), m_ref, v_ref, f_ref, mask)

    @pl.when(n1 > 0)
    def _():
        finish((1,), m_ref, v_ref, f_ref, mask)


def jacobi(counts, stats):
    slots, size, _ = stats.shape
    vm = pl.BlockSpec(memory_space=pltpu.VMEM)
    sm = pl.BlockSpec(memory_space=pltpu.SMEM)
    return pl.pallas_call(
        jacobi_kernel,
        out_shape=(
            jax.ShapeDtypeStruct((slots, size, size), bf16),
            jax.ShapeDtypeStruct((MAXS, slots), f32),
        ),
        in_specs=[sm, vm],
        out_specs=(vm, sm),
        scratch_shapes=[
            pltpu.VMEM((slots, size, size), f32),
            pltpu.VMEM((slots, size, size), f32),
            pltpu.VMEM((slots, size, size), f32),
            pltpu.VMEM((2 * slots, GW, GW), f32),
            pltpu.VMEM((2 * slots, GW, GW), f32),
        ],
        compiler_params=pltpu.CompilerParams(vmem_limit_bytes=48 << 20),
        name="jacobi",
    )(counts, stats)


BLK = ("blk_0", "blk_1", "blk_2")
BLK_GRP = ("blk_0", "blk_1", "blk_2", "grp")


def per_device(statistics, gradients, live_counts, slot_row, sweeps):
    matrices = statistics[0]
    slot_count, block_size, _ = matrices.shape
    row_count = gradients.shape[1]
    blk_rank = lax.axis_index(BLK)
    own_live = lax.dynamic_index_in_dim(live_counts[0], blk_rank, 0, keepdims=False)
    counts = jnp.where(lax.iota(jnp.int32, slot_count) < own_live, sweeps[0], 0)
    factors, offs = jacobi(counts, matrices)
    off_max = lax.pmax(jnp.max(offs, axis=1), BLK_GRP)
    row_ids = lax.iota(jnp.int32, row_count)
    devices = live_counts.shape[1]
    slot_total = devices * slot_count
    slot_ids = lax.iota(jnp.int32, slot_total)
    is_live = slot_ids % slot_count < jnp.repeat(live_counts[0], slot_count)
    matches = (slot_row[0][None, :] == row_ids[:, None]) & is_live[None, :]
    slot_of = jnp.sum(jnp.where(matches, slot_ids[None, :], 0), axis=1)
    piece = block_size // devices
    spread = lax.all_to_all(
        factors.reshape(slot_count, devices, piece, block_size), BLK, 1, 0, tiled=False
    )
    spread = spread.reshape(slot_total, piece, block_size)
    own = jnp.take(spread, slot_of, axis=0)
    chosen = lax.all_gather(own, BLK, axis=1, tiled=True)
    updates = jnp.einsum("kij,kjc->kic", chosen, gradients[0], preferred_element_type=f32)
    return (updates.astype(bf16)[None], off_max)


def solution(mesh):
    split_mesh = Mesh(
        mesh.devices.reshape(4, 4, 2, mesh.shape["grp"]), ("blk_0", "blk_1", "blk_2", "grp")
    )
    return jax.shard_map(
        per_device,
        mesh=split_mesh,
        in_specs=(
            P("grp", BLK, None, None),
            P("grp", None, None, BLK),
            P("grp", None),
            P("grp", None),
            P("grp", BLK),
        ),
        out_specs=(P("grp", None, None, BLK), P()),
        check_vma=False,
    )
```

time: 1800 us -> 177 us (0.10)
  blocking collectives: 1220 us -> 63.8 us
  other arithmetic: 282 us -> 3.02 us
  local copies, waits for them, and re-layouts: 112 us -> 5.29 us
  starting transfers between devices: 0.04 us -> 61.3 us
  waiting for transfers between devices: 69.4 us -> 15.2 us
  matrix products: 44 us -> 11.5 us
  loops' own time: 32.1 us -> 0 us
    pmax x4 -> x1, blocking collectives: 1220 us -> 63.8 us  [per_device(): off_max = lax.pmax(jnp.max(offs, axis=1), BLK_GRP)]
    another operation x36 -> x0, other arithmetic: 266 us -> none  [the longest x9 71.5 us: rotation_of(): left_factor = jnp.linalg.cholesky(identity + 0.25 * outer)]
    all_gather x1, waiting for transfers between devices: 69.4 us -> 0.01 us  [per_device(): chosen = lax.all_gather(own, BLK, axis=1, tiled=True)]
    all_to_all x0 -> x1, starting transfers between devices: none -> 61.3 us  [per_device(): lax.all_to_all(factors.reshape(slot_count, devices, piece, block_size), B...]
    another operation x5 -> x1, local copies, waits for them, and re-layouts: 52.8 us -> 1.07 us  [per_device(): lax.all_to_all(factors.reshape(slot_count, devices, piece, block_size), B...]
    another operation x4 -> x0, loops' own time: 32.1 us -> none  [per_device(): lax.cond(active, one_sweep, keep_both, states[slot_index], eigen_bases[sl...]
    gather x6 -> x1, local copies, waits for them, and re-layouts: 30.6 us -> 0.56 us  [per_device(): own = jnp.take(spread, slot_of, axis=0)]
    dot_general x18 -> x1, matrix products: 38.4 us -> 11.5 us  [per_device(): jnp.einsum('kij,kjc->kic', chosen, gradients[0], preferred_element_type=f32)]
  transfers between devices with their start and end apart: 1 -> 2, of which waited for: 1 -> 1; matrix products, arithmetic and copies ran while one was open for 0% -> 1% of each run, Pallas kernels for 0% -> 0%
where the time goes in v1:
time: 177 us; the launch traced here: 176 us
  blocking collectives  63.8 us (36%)
  starting transfers between devices  61.3 us (35%)
  waiting for transfers between devices  15.2 us (9%)
  between operations  14.1 us (8%)
  matrix products  11.5 us (6%)
  local copies, waits for them, and re-layouts  5.29 us (3%)
  other arithmetic  3.02 us (2%)
    pmax x1, blocking collectives, per_device(): off_max = lax.pmax(jnp.max(offs, axis=1), BLK_GRP)  63.8 us
    all_to_all x1, starting transfers between devices, per_device(): lax.all_to_all(factors.reshape(slot_count, devices, piece, block_size), B...  61.3 us
    all_to_all x1, waiting for transfers between devices, per_device(): lax.all_to_all(factors.reshape(slot_count, devices, piece, block_size), B...  15.2 us
    dot_general x1, matrix products, per_device(): jnp.einsum('kij,kjc->kic', chosen, gradients[0], preferred_element_type=f32)  11.5 us
  transfers between devices with their start and end apart: 2, of which 1 were waited for; matrix products, arithmetic and copies ran while one was open for 1% of the time, Pallas kernels for 0%

profile of v1, /device:TPU:1, one launch (start us, length us, event | category | flops | bytes accessed | tf_op | source)
XLA Modules:
  0.0 175.6 jit_solution(14705024883030425698)
XLA Ops:
  7.2 1.2 constant_dynamic-slice_fusion
  8.4 1.3 compare_select_fusion.2.counts_ref
  9.7 0.0 copy-start
  9.7 1.6 copy-done
  11.3 1.4 jacobi.1
  12.7 1.1 copy.9
  13.8 61.3 %all-to-all-start = ((bf16[1,2,32,16,512]{4,3,1,0,2:T(8,128)(2,1)}), bf16[1,2,32,16,512]{4,3,1,0,2:T(8,128)(2,1)S(1)}, u32[]{:S(2)}, u32[]{:S(2)}) async-start(bf16[1,2,32,16,512]{4,3,1,0,2:T(8,128)(2,1)} %copy.9), calls=%async_computation | async-start | bytes 2097152 | tf_op jit(solution)/shard_map/all_to_all | solution.py:223
  75.1 0.0 all-gather.2.cloned.1.call-start
  75.1 0.7 broadcast_in_dim.35
  75.8 0.1 reshape.42
  75.9 0.8 select_reduce_fusion
  76.8 15.2 %all-to-all-done = bf16[1,2,32,16,512]{4,3,1,0,2:T(8,128)(2,1)S(1)} async-done(((bf16[1,2,32,16,512]{4,3,1,0,2:T(8,128)(2,1)}), bf16[1,2,32,16,512]{4,3,1,0,2:T(8,128)(2,1)S(1)}, u32[]{:S(2)}, u32[]{:S(2)}) %all-to-all-start) | async-done | bytes 1048608 | tf_op jit(solution)/shard_map/all_to_all | solution.py:223
  92.0 0.6 gather_fusion
  92.5 0.8 broadcast_select_fusion
  93.3 0.0 all-gather.2.cloned.1.call-update
  93.4 0.1 reduce_max.9
  93.5 63.8 %pmax.7 = f32[2]{0:T(128)} all-reduce(f32[2]{0:T(128)S(1)} %reduce_max.9), channel_id=1, replica_groups=mesh['blk_0'=4,'blk_1'=4,'blk_2'=2,'grp'=4] {'blk_0','blk_1','blk_2','grp'}, use_global_device_ids=true, to_apply=%region_2.3 | all-reduce | flops 2 | bytes 16 | tf_op jit(solution)/shard_map/pmax | solution.py:214
  157.3 0.0 all-gather.2.cloned.1.call-done
  157.3 11.5 %convert_bitcast_fusion = bf16[1,16,512,448]{2,3,1,0:T(8,128)(2,1)} fusion(bf16[16,512,512]{2,1,0:T(8,128)(2,1)} %all-gather.2.cloned.1.call-done, bf16[1,16,512,448]{2,3,1,0:T(8,128)(2,1)} %param.6), kind=kOutput, calls=%fused_computation.3 | convolution fusion | flops 3761766400 | bytes 23068672 | tf_op jit(solution)/shard_map/kij,kjc->kic/dot_general | solution.py:229
  (4 shorter events, 0.0 us)
Async XLA Ops:
  9.7 1.6 copy-start
  13.8 78.2 %all-to-all-start = ((bf16[1,2,32,16,512]{4,3,1,0,2:T(8,128)(2,1)}), bf16[1,2,32,16,512]{4,3,1,0,2:T(8,128)(2,1)S(1)}, u32[]{:S(2)}, u32[]{:S(2)}) async-start(bf16[1,2,32,16,512]{4,3,1,0,2:T(8,128)(2,1)} %copy.9), calls=%async_computation | async-start | bytes 2097152 | tf_op jit(solution)/shard_map/all_to_all | solution.py:223
  75.1 82.2 %all-gather.2.cloned.1.call-start = ((), (), s32[]{:S(2)}) async-start(), calls=%async_computation.1 | async-start | bytes 8650752 | tf_op jit(solution)/shard_map/all_gather | solution.py:228
Sparse Core Ops, SparseCore 0:
  93.5 48.8 all-gather.1

commit v2 on v1

--- a/solution.py
+++ b/solution.py
@@ -14,6 +14,7 @@
 f32, bf16 = jnp.float32, jnp.bfloat16
 TOL = 1e-6
 DOUBLINGS = 4
+TILES = [(i, j) for i in range(4) for j in range(i, 4)]
 
 
 def split(x):
@@ -122,30 +123,64 @@
 
 
 def finish(slots, m_ref, v_ref, f_ref, mask):
+    dot = functools.partial(
+        lax.dot_general, dimension_numbers=(((1,), (1,)), ((), ())), preferred_element_type=f32
+    )
     for s in slots:
         diagonal = jnp.sum(jnp.where(mask, m_ref[s], 0.0), axis=0, keepdims=True)
         eighth = jnp.sqrt(lax.rsqrt(jnp.sqrt(diagonal)))
         hi, lo = split(v_ref[s] * eighth)
-        dot = functools.partial(
-            lax.dot_general, dimension_numbers=(((1,), (1,)), ((), ())), preferred_element_type=f32
-        )
-        f_ref[s] = (dot(hi, hi) + (dot(lo, hi) + dot(hi, lo))).astype(bf16)
-
-
-def jacobi_kernel(counts_ref, stats_ref, f_ref, off_ref, m_ref, v_ref, y_ref, t_ref, p_ref):
+        for i in range(4):
+            ah, al, bh, bl = hi[grp(i)], lo[grp(i)], hi[i * GW :], lo[i * GW :]
+            line = (dot(ah, bh) + (dot(al, bh) + dot(ah, bl))).astype(bf16)
+            for j in range(i, 4):
+                t = TILES.index((i, j))
+                f_ref[s, grp(t), :] = line[:, grp(j - i)]
+
+
+def note_off(off_ref, i, value):
+    rows = lax.broadcasted_iota(jnp.int32, off_ref.shape, 0)
+    off_ref[...] = jnp.where(rows == i, jnp.maximum(off_ref[...], value), off_ref[...])
+
+
+def jacobi_kernel(
+    live_ref, row_ref, sweeps_ref, stats_ref,
+    f_ref, off_ref, place_ref, m_ref, v_ref, y_ref, t_ref, p_ref, sem,
+):
     size = stats_ref.shape[1]
+    devices = live_ref.shape[0]
     mask = eye_mask(size)
-    n0, n1 = counts_ref[0], counts_ref[1]
-    for i in range(MAXS):
-        for s in range(2):
-            off_ref[i, s] = 0.0
+    rank = (lax.axis_index("blk_0") * 4 + lax.axis_index("blk_1")) * 2 + lax.axis_index("blk_2")
+    own = live_ref[rank]
+    n0 = jnp.where(own > 0, sweeps_ref[0], 0)
+    n1 = jnp.where(own > 1, sweeps_ref[1], 0)
+
+    def load(s):
+        return pltpu.make_async_copy(stats_ref.at[s], m_ref.at[s], sem.at[s])
+
+    for s, n in enumerate((n0, n1)):
+        pl.when(n > 0)(lambda s=s: load(s).start())
+
+    for k in range(place_ref.shape[0]):
+        place_ref[k] = 0
+
+    def note_place(j, carry):
+        @pl.when(lax.rem(j, 2) < live_ref[j // 2])
+        def _():
+            place_ref[row_ref[j]] = lax.rem(j // 2, 2) * devices + (j // 4) * 2 + lax.rem(j, 2)
+
+        return carry
+
+    lax.fori_loop(0, 2 * devices, note_place, 0)
+    off_ref[...] = jnp.zeros_like(off_ref)
     scratch = (m_ref, v_ref, y_ref, t_ref, p_ref)
 
-    @pl.when(n0 > 0)
-    def _():
-        m_ref[...] = stats_ref[...]
-        for s in range(2):
+    for s, n in enumerate((n0, n1)):
+
+        @pl.when(n > 0)
+        def _(s=s):
             v_ref[s] = mask.astype(f32)
+            load(s).wait()
 
     def sweep(i, carry):
         a0, a1 = n0 > i, n1 > i
@@ -154,13 +189,13 @@
         @pl.when(a0 & a1)
         def _():
             sweep_body((0, 1), *scratch)
-            off_ref[i, 0] = off_norm(m_ref[0], eye_mask(size))
-            off_ref[i, 1] = off_norm(m_ref[1], eye_mask(size))
+            for s in range(2):
+                note_off(off_ref, i, off_norm(m_ref[s], eye_mask(size)))
 
         @pl.when(a0 != a1)
         def _():
             sweep_body((slot,), *scratch)
-            off_ref[i, slot] = off_norm(m_ref[slot], eye_mask(size))
+            note_off(off_ref, i, off_norm(m_ref[slot], eye_mask(size)))
 
         return carry
 
@@ -175,67 +210,373 @@
         finish((1,), m_ref, v_ref, f_ref, mask)
 
 
-def jacobi(counts, stats):
+def jacobi(live, slot_row, sweeps, blocks, stats):
     slots, size, _ = stats.shape
     vm = pl.BlockSpec(memory_space=pltpu.VMEM)
     sm = pl.BlockSpec(memory_space=pltpu.SMEM)
     return pl.pallas_call(
         jacobi_kernel,
         out_shape=(
-            jax.ShapeDtypeStruct((slots, size, size), bf16),
-            jax.ShapeDtypeStruct((MAXS, slots), f32),
+            jax.ShapeDtypeStruct((slots, len(TILES) * GW, GW), bf16),
+            jax.ShapeDtypeStruct((8, GW), f32),
+            jax.ShapeDtypeStruct((blocks,), jnp.int32),
         ),
-        in_specs=[sm, vm],
-        out_specs=(vm, sm),
+        in_specs=[sm, sm, sm, pl.BlockSpec(memory_space=pl.ANY)],
+        out_specs=(vm, vm, sm),
         scratch_shapes=[
             pltpu.VMEM((slots, size, size), f32),
             pltpu.VMEM((slots, size, size), f32),
             pltpu.VMEM((slots, size, size), f32),
             pltpu.VMEM((2 * slots, GW, GW), f32),
             pltpu.VMEM((2 * slots, GW, GW), f32),
+            pltpu.SemaphoreType.DMA((2,)),
         ],
         compiler_params=pltpu.CompilerParams(vmem_limit_bytes=48 << 20),
         name="jacobi",
-    )(counts, stats)
-
-
-BLK = ("blk_0", "blk_1", "blk_2")
-BLK_GRP = ("blk_0", "blk_1", "blk_2", "grp")
-
-
-def per_device(statistics, gradients, live_counts, slot_row, sweeps):
+    )(live, slot_row, sweeps, stats)
+
+
+AXES = ("blk_0", "blk_1", "blk_2", "grp")
+CHUNKS = 4
+MESH_ID = pl.DeviceIdType.MESH
+
+
+def gather_kernel(ny, idx_ref, f_ref, off_ref, out_ref, omax_ref,
+                  spread, g, offs, ostage,
+                  s1, r1, s2, r2, sa, ra, sb, rb, sc, rc, sd, rd, se, re,
+                  so, ro, sp, rp, sq, rq, lsem):
+    x, z, e, y = [lax.axis_index(a) for a in AXES]
+    chip = x * 4 + z
+    rows = f_ref.shape[1] // 16
+
+    def ident(c, core, yy):
+        return (c // 4, lax.rem(c, 4), core, yy)
+
+    def remote(src, dst, send, recv, dev):
+        return pltpu.make_async_remote_copy(
+            src_ref=src, dst_ref=dst, send_sem=send, recv_sem=recv,
+            device_id=dev, device_id_type=MESH_ID,
+        )
+
+    twin = ident(chip, 1 - e, y)
+
+    def peer(d):
+        return ident(lax.rem(chip + d, 16), e, y)
+
+    def level(d):
+        return ident(chip, e, lax.rem(y + d, ny))
+
+    barrier = pltpu.get_barrier_semaphore()
+
+    def greet(d, carry):
+        pl.semaphore_signal(barrier, inc=1, device_id=peer(d), device_id_type=MESH_ID)
+        return carry
+
+    lax.fori_loop(1, 16, greet, 0)
+    for d in range(1, ny):
+        pl.semaphore_signal(barrier, inc=1, device_id=level(d), device_id_type=MESH_ID)
+    pl.semaphore_signal(barrier, inc=1, device_id=twin, device_id_type=MESH_ID)
+    pl.semaphore_wait(barrier, 15 + (ny - 1) + 1)
+
+    def my_rows(c):
+        return f_ref.at[:, pl.ds(pl.multiple_of(c * rows, 16), rows), :]
+
+    def spread_copy(d):
+        target = lax.rem(chip + d, 16)
+        return remote(my_rows(target), spread.at[e, chip], s1.at[d], r1.at[d], peer(d))
+
+    def pass_copy(d):
+        source = lax.rem(chip + 16 - d, 16)
+        return remote(spread.at[e, source], spread.at[e, source], s2.at[d], r2.at[d], twin)
+
+    def own_copy():
+        return remote(my_rows(chip), spread.at[e, chip], s2.at[0], r2.at[0], twin)
+
+    def off_copy(d):
+        return remote(off_ref, offs.at[d], so.at[d], ro.at[d], peer(d))
+
+    def go(copy):
+        def step(d, carry):
+            copy(d).start()
+            return carry
+        return step
+
+    lax.fori_loop(1, 16, go(spread_copy), 0)
+    lax.fori_loop(1, 16, go(off_copy), 0)
+    own_copy().start()
+    spread[e, chip] = f_ref[:, pl.ds(pl.multiple_of(chip * rows, 16), rows), :]
+    offs[0] = off_ref[...]
+
+    def relay_twin(d, carry):
+        source = lax.rem(chip + 16 - d, 16)
+        remote(my_rows(chip), spread.at[e, source], s1.at[d], r1.at[d], peer(d)).wait_recv()
+        pass_copy(d).start()
+        return carry
+
+    lax.fori_loop(1, 16, relay_twin, 0)
+
+    def twin_in(d, carry):
+        source = lax.rem(chip + 16 - d, 16)
+        remote(
+            spread.at[1 - e, source], spread.at[1 - e, source], s2.at[d], r2.at[d], twin
+        ).wait_recv()
+        return carry
+
+    lax.fori_loop(0, 16, twin_in, 0)
+
+    for q in range(CHUNKS):
+        for b in range(2):
+            k = 4 * q + 2 * e + b
+            j = idx_ref[k]
+            g[chip, k] = spread[j // 32, lax.rem(j, 32) // 2, lax.rem(j, 2)]
+
+    pos1 = jnp.where(e == 0, x, z)
+    pos2 = jnp.where(e == 0, z, x)
+
+    def at(p1, p2):
+        p1, p2 = lax.rem(p1, 4), lax.rem(p2, 4)
+        return jnp.where(e == 0, p1 * 4 + p2, p2 * 4 + p1)
+
+    def pair(c, q):
+        return g.at[c, pl.ds(4 * q + 2 * e, 2)]
+
+    def single(c, q, b):
+        return g.at[c, pl.ds(4 * q + 2 * e + b, 1)]
+
+    def first(q, w):
+        dev = ident(at(pos1 + 1 + 2 * w, pos2), e, y)
+        return remote(pair(chip, q), pair(chip, q), sa.at[q, w], ra.at[q, w], dev)
+
+    def first_in(q, w):
+        c = at(pos1 + 3 - 2 * w, pos2)
+        return remote(pair(c, q), pair(c, q), sa.at[q, w], ra.at[q, w], twin)
+
+    def second(q, w):
+        c = at(pos1 + 3 - 2 * w, pos2)
+        dev = ident(at(pos1 + 1 + 2 * w, pos2), e, y)
+        return remote(single(c, q, w), single(c, q, w), sb.at[q, w], rb.at[q, w], dev)
+
+    def second_in(q, w):
+        c = at(pos1 + 2, pos2)
+        return remote(single(c, q, w), single(c, q, w), sb.at[q, w], rb.at[q, w], twin)
+
+    def third(q, o, w):
+        c = at(pos1 + o, pos2)
+        dev = ident(at(pos1, pos2 + 1 + 2 * w), e, y)
+        return remote(pair(c, q), pair(c, q), sc.at[q, o, w], rc.at[q, o, w], dev)
+
+    def third_in(q, o, w):
+        c = at(pos1 + o, pos2 + 3 - 2 * w)
+        return remote(pair(c, q), pair(c, q), sc.at[q, o, w], rc.at[q, o, w], twin)
+
+    def fourth(q, o, w):
+        c = at(pos1 + o, pos2 + 3 - 2 * w)
+        dev = ident(at(pos1, pos2 + 1 + 2 * w), e, y)
+        return remote(single(c, q, w), single(c, q, w), sd.at[q, o, w], rd.at[q, o, w], dev)
+
+    def fourth_in(q, o, w):
+        c = at(pos1 + o, pos2 + 2)
+        return remote(single(c, q, w), single(c, q, w), sd.at[q, o, w], rd.at[q, o, w], twin)
+
+    def across(q, core):
+        part = g.at[:, pl.ds(4 * q + 2 * core, 2)]
+        return remote(part, part, se.at[q], re.at[q], twin)
+
+    def out_copy(q):
+        part = (slice(None), pl.ds(4 * q, 4))
+        return pltpu.make_async_copy(g.at[part], out_ref.at[part], lsem.at[q])
+
+    def wave0(q, carry):
+        for w in range(2):
+            first(q, w).start()
+            third(q, 0, w).start()
+        return carry
+
+    def wave1(q, carry):
+        for w in range(2):
+            first_in(q, w).wait_recv()
+            second(q, w).start()
+        for w in range(2):
+            third(q, 1, w).start()
+            third(q, 3, w).start()
+        for w in range(2):
+            third_in(q, 0, w).wait_recv()
+            fourth(q, 0, w).start()
+        return carry
+
+    def wave2(q, carry):
+        for w in range(2):
+            second_in(q, w).wait_recv()
+        for w in range(2):
+            third(q, 2, w).start()
+        for o in (1, 3):
+            for w in range(2):
+                third_in(q, o, w).wait_recv()
+                fourth(q, o, w).start()
+        return carry
+
+    def wave3(q, carry):
+        for w in range(2):
+            third_in(q, 2, w).wait_recv()
+            fourth(q, 2, w).start()
+        return carry
+
+    def wave4(q, carry):
+        for o in range(4):
+            for w in range(2):
+                fourth_in(q, o, w).wait_recv()
+        across(q, e).start()
+        return carry
+
+    def wave5(q, carry):
+        across(q, 1 - e).wait_recv()
+        out_copy(q).start()
+        return carry
+
+    def off_in(d, carry):
+        remote(off_ref, offs.at[d], so.at[d], ro.at[d], peer(d)).wait_recv()
+        return carry
+
+    lax.fori_loop(1, 16, off_in, 0)
+    top = offs[0]
+    for d in range(1, 16):
+        top = jnp.maximum(top, offs[d])
+    ostage[0] = top
+
+    def level_copy(d):
+        return remote(ostage.at[0], ostage.at[d], sp.at[d], rp.at[d], level(d))
+
+    lax.fori_loop(0, CHUNKS, wave0, 0)
+    for d in range(1, ny):
+        level_copy(d).start()
+
+    lax.fori_loop(0, CHUNKS, wave1, 0)
+
+    for d in range(1, ny):
+        level_copy(d).wait_recv()
+        top = jnp.maximum(top, ostage[d])
+    ostage[ny] = top
+
+    def core_copy():
+        return remote(ostage.at[ny], ostage.at[ny + 1], sq, rq, twin)
+
+    lax.fori_loop(0, CHUNKS, wave2, 0)
+    core_copy().start()
+    lax.fori_loop(0, CHUNKS, wave3, 0)
+    core_copy().wait_recv()
+    omax_ref[...] = jnp.maximum(top, ostage[ny + 1])
+    lax.fori_loop(0, CHUNKS, wave4, 0)
+    lax.fori_loop(0, CHUNKS, wave5, 0)
+
+    own_copy().wait_send()
+
+    def drain(d, carry):
+        spread_copy(d).wait_send()
+        pass_copy(d).wait_send()
+        off_copy(d).wait_send()
+        return carry
+
+    lax.fori_loop(1, 16, drain, 0)
+    for d in range(1, ny):
+        level_copy(d).wait_send()
+    core_copy().wait_send()
+
+    def drain_chunk(q, carry):
+        for w in range(2):
+            first(q, w).wait_send()
+            second(q, w).wait_send()
+            for o in range(4):
+                third(q, o, w).wait_send()
+                fourth(q, o, w).wait_send()
+        across(q, e).wait_send()
+        out_copy(q).wait()
+        return carry
+
+    lax.fori_loop(0, CHUNKS, drain_chunk, 0)
+
+
+def gather(idx, packed, offs, ny):
+    slots, length, width = packed.shape
+    rows = length // 16
+    blocks = idx.shape[0]
+    vm = pl.BlockSpec(memory_space=pltpu.VMEM)
+    dma = pltpu.SemaphoreType.DMA
+    n = CHUNKS
+    return pl.pallas_call(
+        functools.partial(gather_kernel, ny),
+        out_shape=(
+            jax.ShapeDtypeStruct((16, blocks, rows, width), bf16),
+            jax.ShapeDtypeStruct(offs.shape, f32),
+        ),
+        in_specs=[pl.BlockSpec(memory_space=pltpu.SMEM), vm, vm],
+        out_specs=(pl.BlockSpec(memory_space=pl.ANY), vm),
+        scratch_shapes=[
+            pltpu.VMEM((2, 16, slots, rows, width), bf16),
+            pltpu.VMEM((16, blocks, rows, width), bf16),
+            pltpu.VMEM((16,) + offs.shape, f32),
+            pltpu.VMEM((ny + 2,) + offs.shape, f32),
+            dma((16,)), dma((16,)), dma((16,)), dma((16,)),
+            dma((n, 2)), dma((n, 2)), dma((n, 2)), dma((n, 2)),
+            dma((n, 4, 2)), dma((n, 4, 2)), dma((n, 4, 2)), dma((n, 4, 2)),
+            dma((n,)), dma((n,)),
+            dma((16,)), dma((16,)), dma((ny,)), dma((ny,)), dma, dma,
+            dma((n,)),
+        ],
+        compiler_params=pltpu.CompilerParams(
+            collective_id=0, has_side_effects=True, vmem_limit_bytes=32 << 20
+        ),
+        name="gather_factors",
+    )(idx, packed, offs)
+
+
+def apply_kernel(p_ref, g_ref, u_ref):
+    count, _, rows, width = p_ref.shape
+    packed = p_ref[...].reshape(count * rows, width)
+    tiles = {ij: packed[t * GW : (t + 1) * GW] for t, ij in enumerate(TILES)}
+    lines = [
+        jnp.concatenate([tiles[i, j] if j >= i else tiles[j, i].T for j in range(4)], axis=1)
+        for i in range(4)
+    ]
+    u_ref[0] = jnp.dot(
+        g_ref[0], jnp.concatenate(lines, axis=0), preferred_element_type=f32
+    ).astype(bf16)
+
+
+def apply(packed, gradients):
+    blocks, cols, size = gradients.shape
+    chips, _, rows, width = packed.shape
+    return pl.pallas_call(
+        apply_kernel,
+        grid=(blocks,),
+        out_shape=jax.ShapeDtypeStruct((blocks, cols, size), bf16),
+        in_specs=[
+            pl.BlockSpec((chips, 1, rows, width), lambda k: (0, k, 0, 0)),
+            pl.BlockSpec((1, cols, size), lambda k: (k, 0, 0)),
+        ],
+        out_specs=pl.BlockSpec((1, cols, size), lambda k: (k, 0, 0)),
+        compiler_params=pltpu.CompilerParams(vmem_limit_bytes=32 << 20),
+        name="apply_factors",
+    )(packed, gradients)
+
+
+BLK = AXES[:3]
+
+
+def per_device(ny, statistics, gradients, live_counts, slot_row, sweeps):
     matrices = statistics[0]
-    slot_count, block_size, _ = matrices.shape
-    row_count = gradients.shape[1]
-    blk_rank = lax.axis_index(BLK)
-    own_live = lax.dynamic_index_in_dim(live_counts[0], blk_rank, 0, keepdims=False)
-    counts = jnp.where(lax.iota(jnp.int32, slot_count) < own_live, sweeps[0], 0)
-    factors, offs = jacobi(counts, matrices)
-    off_max = lax.pmax(jnp.max(offs, axis=1), BLK_GRP)
-    row_ids = lax.iota(jnp.int32, row_count)
-    devices = live_counts.shape[1]
-    slot_total = devices * slot_count
-    slot_ids = lax.iota(jnp.int32, slot_total)
-    is_live = slot_ids % slot_count < jnp.repeat(live_counts[0], slot_count)
-    matches = (slot_row[0][None, :] == row_ids[:, None]) & is_live[None, :]
-    slot_of = jnp.sum(jnp.where(matches, slot_ids[None, :], 0), axis=1)
-    piece = block_size // devices
-    spread = lax.all_to_all(
-        factors.reshape(slot_count, devices, piece, block_size), BLK, 1, 0, tiled=False
+    packed, offs, where_of = jacobi(
+        live_counts[0], slot_row[0], sweeps[0], gradients.shape[1], matrices
     )
-    spread = spread.reshape(slot_total, piece, block_size)
-    own = jnp.take(spread, slot_of, axis=0)
-    chosen = lax.all_gather(own, BLK, axis=1, tiled=True)
-    updates = jnp.einsum("kij,kjc->kic", chosen, gradients[0], preferred_element_type=f32)
-    return (updates.astype(bf16)[None], off_max)
+    pieces, tops = gather(where_of, packed, offs, ny)
+    updates = apply(pieces, jnp.swapaxes(gradients[0], 1, 2))
+    return jnp.swapaxes(updates, 1, 2)[None], tops[:MAXS, 0]
 
 
 def solution(mesh):
-    split_mesh = Mesh(
-        mesh.devices.reshape(4, 4, 2, mesh.shape["grp"]), ("blk_0", "blk_1", "blk_2", "grp")
-    )
+    ny = mesh.shape["grp"]
+    split_mesh = Mesh(mesh.devices.reshape(4, 4, 2, ny), AXES)
     return jax.shard_map(
-        per_device,
+        functools.partial(per_device, ny),
         mesh=split_mesh,
         in_specs=(
             P("grp", BLK, None, None),

time: 177 us -> 117 us (0.66); the launches traced: 176 us -> 118 us
  Pallas kernels: 1.4 us -> 110 us
  blocking collectives: 63.8 us -> 0 us
  starting transfers between devices: 61.3 us -> 0 us
  waiting for transfers between devices: 15.2 us -> 0 us
  between operations: 14.1 us -> 0.66 us
  matrix products: 11.5 us -> 0 us
  other arithmetic: 3.02 us -> 0 us
  local copies, waits for them, and re-layouts: 5.29 us -> 7.26 us
    pallas_call x1 -> x3, Pallas kernels: 1.4 us -> 110 us  [the longest x1 79.5 us: gather(): pl.pallas_call(functools.partial(gather_kernel, ny), out_shape=(jax.Shape...]
    pmax x1 -> x0, blocking collectives: 63.8 us -> none  [per_device(): off_max = lax.pmax(jnp.max(offs, axis=1), BLK_GRP)]
    all_to_all x1 -> x0, starting transfers between devices: 61.3 us -> none  [per_device(): lax.all_to_all(factors.reshape(slot_count, devices, piece, block_size), B...]
    all_to_all x1 -> x0, waiting for transfers between devices: 15.2 us -> none  [per_device(): lax.all_to_all(factors.reshape(slot_count, devices, piece, block_size), B...]
    dot_general x1 -> x0, matrix products: 11.5 us -> none  [per_device(): jnp.einsum('kij,kjc->kic', chosen, gradients[0], preferred_element_type=f32)]
    unnamed x2 -> x10, local copies, waits for them, and re-layouts: 1.59 us -> 6.63 us
    select_n x3 -> x0, other arithmetic: 2.11 us -> none  [the longest x1 1.3 us: per_device(): counts = jnp.where(lax.iota(jnp.int32, slot_count) < own_live, sweeps[0], 0)]
  transfers between devices with their start and end apart: 2 -> 0, of which waited for: 1 -> 0; matrix products, arithmetic and copies ran while one was open for 1% -> 0% of each run, Pallas kernels for 0% -> 0%
where the time goes in v2:
time: 117 us; the launch traced here: 118 us
  Pallas kernels  110 us (94%)
  local copies, waits for them, and re-layouts  7.26 us (6%)
    pallas_call x1, Pallas kernels, gather(): pl.pallas_call(functools.partial(gather_kernel, ny), out_shape=(jax.Shape...  79.5 us
    pallas_call x1, Pallas kernels, jacobi(): pl.pallas_call(jacobi_kernel, out_shape=(jax.ShapeDtypeStruct((slots, len...  20.1 us
    pallas_call x1, Pallas kernels, apply(): pl.pallas_call(apply_kernel, grid=(blocks,), out_shape=jax.ShapeDtypeStru...  10.3 us
    unnamed x10, local copies, waits for them, and re-layouts  6.63 us

profile of v2, /device:TPU:1, one launch (start us, length us, event | category | flops | bytes accessed | tf_op | source)
XLA Modules:
  0.0 117.8 jit_solution(14329899758612764809)
XLA Ops:
  0.6 0.0 copy-start.1
  0.6 1.6 %copy-done.1 = f32[1,2,512,512]{3,2,1,0:T(8,128)S(1)} copy-done((f32[1,2,512,512]{3,2,1,0:T(8,128)S(1)}, f32[1,2,512,512]{3,2,1,0:T(8,128)}, u32[]{:S(2)}) %copy-start.1) | copy-done | bytes 2097176
  2.2 0.0 copy-start.2
  2.2 0.7 copy-done.2
  2.9 0.0 copy-start.3
  2.9 0.7 copy-done.3
  3.5 0.0 copy-start.4
  3.5 0.7 copy-done.4
  4.2 20.1 %jacobi.1 = (bf16[2,1280,128]{2,1,0:T(8,128)(2,1)S(1)}, f32[8,128]{1,0:T(8,128)S(1)}, s32[16]{0:T(128)S(1)}) custom-call(s32[32]{0:T(128)S(1)} %bitcast.12, s32[64]{0:T(128)S(1)} %bitcast.13, s32[2]{0:T(128)S(1)} %bitcast.14, f32[2,512,512]{2,1,0:T(8,128)S(1)} %bitcast.11), custom_call_target="tpu_custom_call" | custom-call | tf_op jit(solution)/shard_map/jacobi/pallas_call | solution.py:217
  24.3 79.5 %gather_factors.1 = (bf16[16,16,80,128]{3,2,1,0:T(8,128)(2,1)S(1)}, f32[8,128]{1,0:T(8,128)S(1)}) custom-call(s32[16]{0:T(128)S(1)} %get-tuple-element.7.idx_ref, bf16[2,1280,128]{2,1,0:T(8,128)(2,1)S(1)} %get-tuple-element.8.f_ref, f32[8,128]{1,0:T(8,128)S(1)} %get-tuple-element.9.off_ref), custom_call_target="tpu_custom_call" | custom-call | tf_op jit(solution)/shard_map/gather_factors/pallas_call | solution.py:505
  103.8 0.6 slice_reduce_fusion
  104.5 0.0 copy-start
  104.5 3.1 %copy-done = bf16[1,16,512,448]{2,3,1,0:T(8,128)(2,1)S(1)} copy-done((bf16[1,16,512,448]{2,3,1,0:T(8,128)(2,1)S(1)}, bf16[1,16,512,448]{2,3,1,0:T(8,128)(2,1)}, u32[]{:S(2)}) %copy-start) | copy-done | bytes 7340056
  107.5 10.3 %apply_factors.1 = bf16[16,448,512]{2,1,0:T(8,128)(2,1)} custom-call(bf16[16,16,80,128]{3,2,1,0:T(8,128)(2,1)S(1)} %get-tuple-element.10.p_ref, bf16[16,448,512]{2,1,0:T(8,128)(2,1)S(1)} %bitcast.10), custom_call_target="tpu_custom_call" | custom-call | tf_op jit(solution)/shard_map/apply_factors/pallas_call | solution.py:548
Async XLA Ops:
  0.6 1.6 %copy-start.1 = (f32[1,2,512,512]{3,2,1,0:T(8,128)S(1)}, f32[1,2,512,512]{3,2,1,0:T(8,128)}, u32[]{:S(2)}) copy-start(f32[1,2,512,512]{3,2,1,0:T(8,128)} %param.5) | copy-start | bytes 6291460
  2.2 0.7 copy-start.2
  2.9 0.7 copy-start.3
  3.5 0.7 copy-start.4
  104.5 3.1 %copy-start = (bf16[1,16,512,448]{2,3,1,0:T(8,128)(2,1)S(1)}, bf16[1,16,512,448]{2,3,1,0:T(8,128)(2,1)}, u32[]{:S(2)}) copy-start(bf16[1,16,512,448]{2,3,1,0:T(8,128)(2,1)} %param.6) | copy-start | bytes 22020100

commit v3 on v2

--- a/solution.py
+++ b/solution.py
@@ -13,7 +13,7 @@
 pairings = ((0, 1, 2, 3), (0, 2, 1, 3), (0, 3, 1, 2))
 f32, bf16 = jnp.float32, jnp.bfloat16
 TOL = 1e-6
-DOUBLINGS = 4
+EASY = 1.5
 TILES = [(i, j) for i in range(4) for j in range(i, 4)]
 
 
@@ -22,9 +22,29 @@
     return hi, (x - hi.astype(f32)).astype(bf16)
 
 
+def dot(a, b):
+    return jnp.dot(a, b, preferred_element_type=f32)
+
+
 def dot3(a, b):
-    dot = functools.partial(jnp.dot, preferred_element_type=f32)
     return dot(a[0], b[0]) + (dot(a[1], b[0]) + dot(a[0], b[1]))
+
+
+def dot3_packed(a, b):
+    left = jnp.concatenate([a[0], a[1]], axis=1)
+    top = jnp.concatenate([b[0], b[1]], axis=1)
+    low = jnp.concatenate([b[0], jnp.zeros_like(b[1])], axis=1)
+    both = dot(left, jnp.concatenate([top, low], axis=0))
+    return both[:, :GW] + both[:, GW:]
+
+
+def two(a, b):
+    return jnp.concatenate([a, b], axis=1)
+
+
+def apart(pair):
+    blank = jnp.zeros((GW, GW), pair.dtype)
+    return jnp.concatenate([two(pair[:, :GW], blank), two(blank, pair[:, GW:])], axis=0)
 
 
 def grp(member):
@@ -36,84 +56,138 @@
     return rows == lax.broadcasted_iota(jnp.int32, (size, size), 1)
 
 
-def sweep_body(slots, m_ref, v_ref, y_ref, t_ref, p_ref):
+def inverse_rare(jobs, w_ref, b_ref, p_ref, peak):
+    identity = eye_mask(GW).astype(f32)
+    alpha = 2.0 / (2.0 + peak)
+    for j in jobs:
+        c = (1.0 - alpha) * identity - alpha * b_ref[j]
+        p_ref[j] = c
+        w_ref[j] = identity + c
+
+    def more(r):
+        for j in jobs:
+            sp = split(p_ref[j])
+            p = dot3(sp, sp)
+            p_ref[j] = p
+            t = w_ref[j]
+            w_ref[j] = t + dot3(split(t), split(p))
+        return r * r
+
+    rho = peak / (2.0 + peak)
+    lax.while_loop(lambda r: r > TOL, more, rho * rho)
+    for j in jobs:
+        w_ref[j] = alpha * w_ref[j]
+
+
+def sweep_body(slots, m_ref, v_ref, y_ref, w_ref, b_ref, p_ref, r_ref):
     mask = eye_mask(GW)
     identity = mask.astype(f32)
+    eye2 = two(identity, identity)
+
+    def rot(s, h):
+        return (
+            (r_ref[s, h, 0], r_ref[s, h, 1]),
+            (r_ref[s, h, 2], r_ref[s, h, 3]),
+        )
+
+    def block(s, rows, cols):
+        lines = [two(m_ref[s, grp(a), grp(cols[0])], m_ref[s, grp(a), grp(cols[1])]) for a in rows]
+        return jnp.concatenate(lines, axis=0)
+
+    def store(s, rows, cols, value):
+        for i, a in enumerate(rows):
+            for j, b in enumerate(cols):
+                m_ref[s, grp(a), grp(b)] = value[grp(i), grp(j)]
+
+    def settle(s, halves):
+        for h in range(2):
+            r, rt = rot(s, h)
+            store(s, halves[h], halves[h], dot3(rt, split(y_ref[s, h])))
+            cols = two(v_ref[s, :, grp(halves[h][0])], v_ref[s, :, grp(halves[h][1])])
+            turned = dot3(split(cols), r)
+            for i in range(2):
+                v_ref[s, :, grp(halves[h][i])] = turned[:, grp(i)]
+
+    last, diagonals = None, {}
     for pairing in pairings:
-        jobs = [(s, pairing[2 * h], pairing[2 * h + 1]) for s in slots for h in range(2)]
-        angles, alphas = [], []
+        halves = (pairing[:2], pairing[2:])
         peak = None
-        for j, (s, a, b) in enumerate(jobs):
-            low = jnp.sum(jnp.where(mask, m_ref[s, grp(a), grp(a)], 0.0), axis=1, keepdims=True)
-            up = jnp.sum(jnp.where(mask, m_ref[s, grp(b), grp(b)], 0.0), axis=0, keepdims=True)
-            c = m_ref[s, grp(a), grp(b)]
-            diff = up - low
-            both = up + low
-            ang = c * diff / (diff * diff + 4.0 * c * c + damping * (both * both))
-            ang_t = ang.T
-            sa, sat = split(ang), split(ang_t)
-            bb = 0.25 * dot3(sa, sat)
+        kept = {}
+        for n, s in enumerate(slots):
+            ang, mats = [], []
+            for h, (a, b) in enumerate(halves):
+                if last is None:
+                    low = jnp.sum(jnp.where(mask, m_ref[s, grp(a), grp(a)], 0.0), axis=1, keepdims=True)
+                    up = jnp.sum(jnp.where(mask, m_ref[s, grp(b), grp(b)], 0.0), axis=0, keepdims=True)
+                else:
+                    low = jnp.sum(jnp.where(mask, diagonals[n, a], 0.0), axis=1, keepdims=True)
+                    up = diagonals[n, b]
+                c = m_ref[s, grp(a), grp(b)]
+                diff = up - low
+                both = up + low
+                one = c * diff / (diff * diff + 4.0 * c * c + damping * (both * both))
+                sa, sat = split(one), split(one.T)
+                bb = 0.25 * dot3_packed(sa, sat)
+                b_ref[2 * n + h] = bb
+                ang.append((sa, sat))
+                mats.append(bb)
+            bb = two(*mats)
             bound = jnp.max(jnp.sum(jnp.abs(bb), axis=0, keepdims=True), axis=1, keepdims=True)
             alpha = 2.0 / (2.0 + bound)
-            cc = (1.0 - alpha) * identity - alpha * bb
-            sc = split(cc)
-            t = identity + cc
-            p = dot3(sc, sc)
-            for k in range(1, DOUBLINGS):
-                sp = split(p)
-                t = t + dot3(split(t), sp)
-                if k < DOUBLINGS - 1:
-                    p = dot3(sp, sp)
-            t_ref[j] = t
-            p_ref[j] = p
-            angles.append((ang, sa, sat))
-            alphas.append(alpha)
+            c = (1.0 - alpha) * eye2 - alpha * bb
+            cb = c.astype(bf16)
+            p = dot(cb, apart(cb))
+            t = eye2 + c
+            pb = p.astype(bf16)
+            stacked = dot(jnp.concatenate([t.astype(bf16), pb], axis=0), apart(pb))
+            t = t + stacked[:GW]
+            w = alpha * (t + dot(t.astype(bf16), apart(stacked[GW:].astype(bf16))))
+            done = two(*[
+                dot3_packed(split(mats[h]), split(w[:, grp(h)])) for h in range(2)
+            ])
+            error = eye2 - w - done
+            w = w + dot(w.astype(bf16), apart(error.astype(bf16)))
+            for h in range(2):
+                w_ref[2 * n + h] = w[:, grp(h)]
+            kept[n] = ang
             peak = bound if peak is None else jnp.maximum(peak, bound)
-        rho = jnp.max(peak / (2.0 + peak))
-        for _ in range(DOUBLINGS):
-            rho = rho * rho
-
-        def more(r):
-            for j in range(len(jobs)):
-                sp = split(p_ref[j])
-                p = dot3(sp, sp)
-                p_ref[j] = p
-                t = t_ref[j]
-                t_ref[j] = t + dot3(split(t), split(p))
-            return r * r
-
-        lax.while_loop(lambda r: r > TOL, more, rho)
-
-        rots = []
-        for j in range(len(jobs)):
-            ang, sa, sat = angles[j]
-            w = alphas[j] * t_ref[j]
-            x = dot3(split(w), sa)
-            q = identity - 0.5 * dot3(sat, split(x))
-            p = 2.0 * w - identity
-            xt = x.T
-            r = jnp.concatenate(
-                [jnp.concatenate([p, x], axis=1), jnp.concatenate([-xt, q], axis=1)], axis=0
-            )
-            rt = jnp.concatenate(
-                [jnp.concatenate([p, -x], axis=1), jnp.concatenate([xt, q], axis=1)], axis=0
-            )
-            rots.append((split(r), split(rt)))
-        for j, (s, a, b) in enumerate(jobs):
-            cols = jnp.concatenate([m_ref[s, :, grp(a)], m_ref[s, :, grp(b)]], axis=1)
-            y = dot3(split(cols), rots[j][0])
-            y_ref[s, :, grp(a)] = y[:, :GW]
-            y_ref[s, :, grp(b)] = y[:, GW:]
-        for j, (s, a, b) in enumerate(jobs):
-            rows = jnp.concatenate([y_ref[s, grp(a), :], y_ref[s, grp(b), :]], axis=0)
-            z = dot3(rots[j][1], split(rows))
-            m_ref[s, grp(a), :] = z[:GW]
-            m_ref[s, grp(b), :] = z[GW:]
-        for j, (s, a, b) in enumerate(jobs):
-            cols = jnp.concatenate([v_ref[s, :, grp(a)], v_ref[s, :, grp(b)]], axis=1)
-            y = dot3(split(cols), rots[j][0])
-            v_ref[s, :, grp(a)] = y[:, :GW]
-            v_ref[s, :, grp(b)] = y[:, GW:]
+            if last is not None:
+                settle(s, last)
+        peak = jnp.max(peak)
+
+        @pl.when(peak > EASY)
+        def _():
+            inverse_rare(range(2 * len(slots)), w_ref, b_ref, p_ref, peak)
+
+        for n, s in enumerate(slots):
+            for h, (sa, sat) in enumerate(kept[n]):
+                w = w_ref[2 * n + h]
+                x = dot3_packed(split(w), sa)
+                sx = split(x)
+                q = identity - 0.5 * dot3_packed(sat, sx)
+                p = 2.0 * w - identity
+                sp, sq, sxt = split(p), split(q), split(x.T)
+                for i in range(2):
+                    r_ref[s, h, i] = jnp.concatenate([two(sp[i], sx[i]), two(-sxt[i], sq[i])], axis=0)
+                    r_ref[s, h, 2 + i] = jnp.concatenate(
+                        [two(sp[i], -sx[i]), two(sxt[i], sq[i])], axis=0
+                    )
+        for n, s in enumerate(slots):
+            r0, rt0 = rot(s, 0)
+            r1, _ = rot(s, 1)
+            z = dot3(rt0, split(dot3(split(block(s, halves[0], halves[1])), r1)))
+            for h, r in enumerate((r0, r1)):
+                y = dot3(split(block(s, halves[h], halves[h])), r)
+                y_ref[s, h] = y
+                full = r[0].astype(f32) + r[1].astype(f32)
+                row = jnp.sum(full * y, axis=0, keepdims=True)
+                for i in range(2):
+                    diagonals[n, halves[h][i]] = row[:, grp(i)]
+            store(s, halves[0], halves[1], z)
+            store(s, halves[1], halves[0], z.T)
+        last = halves
+    for s in slots:
+        settle(s, last)
 
 
 def off_norm(matrix, mask):
@@ -144,9 +218,20 @@
 
 
 def jacobi_kernel(
-    live_ref, row_ref, sweeps_ref, stats_ref,
-    f_ref, off_ref, place_ref, m_ref, v_ref, y_ref, t_ref, p_ref, sem,
+    live_any, row_any, sweeps_any, stats_ref,
+    f_ref, off_ref, place_ref, m_ref, v_ref, y_ref, w_ref, b_ref, p_ref, r_ref, live_s, row_s, sweeps_s, sem,
 ):
+    small = [
+        pltpu.make_async_copy(src, dst, sem.at[2 + i])
+        for i, (src, dst) in enumerate(
+            ((live_any, live_s), (row_any, row_s), (sweeps_any, sweeps_s))
+        )
+    ]
+    for copy in small:
+        copy.start()
+    for copy in small:
+        copy.wait()
+    live_ref, row_ref, sweeps_ref = live_s.at[0], row_s.at[0], sweeps_s.at[0]
     size = stats_ref.shape[1]
     devices = live_ref.shape[0]
     mask = eye_mask(size)
@@ -173,7 +258,7 @@
 
     lax.fori_loop(0, 2 * devices, note_place, 0)
     off_ref[...] = jnp.zeros_like(off_ref)
-    scratch = (m_ref, v_ref, y_ref, t_ref, p_ref)
+    scratch = (m_ref, v_ref, y_ref, w_ref, b_ref, p_ref, r_ref)
 
     for s, n in enumerate((n0, n1)):
 
@@ -221,30 +306,37 @@
             jax.ShapeDtypeStruct((8, GW), f32),
             jax.ShapeDtypeStruct((blocks,), jnp.int32),
         ),
-        in_specs=[sm, sm, sm, pl.BlockSpec(memory_space=pl.ANY)],
+        in_specs=[pl.BlockSpec(memory_space=pltpu.HBM)] * 4,
         out_specs=(vm, vm, sm),
         scratch_shapes=[
             pltpu.VMEM((slots, size, size), f32),
             pltpu.VMEM((slots, size, size), f32),
-            pltpu.VMEM((slots, size, size), f32),
+            pltpu.VMEM((slots, 2, 2 * GW, 2 * GW), f32),
             pltpu.VMEM((2 * slots, GW, GW), f32),
             pltpu.VMEM((2 * slots, GW, GW), f32),
-            pltpu.SemaphoreType.DMA((2,)),
+            pltpu.VMEM((2 * slots, GW, GW), f32),
+            pltpu.VMEM((slots, 2, 4, 2 * GW, 2 * GW), bf16),
+            pltpu.SMEM(live.shape, jnp.int32),
+            pltpu.SMEM(slot_row.shape, jnp.int32),
+            pltpu.SMEM(sweeps.shape, jnp.int32),
+            pltpu.SemaphoreType.DMA((5,)),
         ],
-        compiler_params=pltpu.CompilerParams(vmem_limit_bytes=48 << 20),
+        cost_estimate=pl.CostEstimate(flops=20 * 10**9, bytes_accessed=1 << 20, transcendentals=0),
+        compiler_params=pltpu.CompilerParams(vmem_limit_bytes=24 << 20),
         name="jacobi",
     )(live, slot_row, sweeps, stats)
 
 
 AXES = ("blk_0", "blk_1", "blk_2", "grp")
 CHUNKS = 4
+WIDE = 8 // CHUNKS
 MESH_ID = pl.DeviceIdType.MESH
 
 
-def gather_kernel(ny, idx_ref, f_ref, off_ref, out_ref, omax_ref,
-                  spread, g, offs, ostage,
+def gather_kernel(ny, idx_ref, f_ref, off_ref, g, omax_ref,
+                  spread, offs, ostage,
                   s1, r1, s2, r2, sa, ra, sb, rb, sc, rc, sd, rd, se, re,
-                  so, ro, sp, rp, sq, rq, lsem):
+                  so, ro, sp, rp, sq, rq):
     x, z, e, y = [lax.axis_index(a) for a in AXES]
     chip = x * 4 + z
     rows = f_ref.shape[1] // 16
@@ -325,8 +417,8 @@
     lax.fori_loop(0, 16, twin_in, 0)
 
     for q in range(CHUNKS):
-        for b in range(2):
-            k = 4 * q + 2 * e + b
+        for b in range(WIDE):
+            k = WIDE * (2 * q + e) + b
             j = idx_ref[k]
             g[chip, k] = spread[j // 32, lax.rem(j, 32) // 2, lax.rem(j, 2)]
 
@@ -338,10 +430,10 @@
         return jnp.where(e == 0, p1 * 4 + p2, p2 * 4 + p1)
 
     def pair(c, q):
-        return g.at[c, pl.ds(4 * q + 2 * e, 2)]
+        return g.at[c, pl.ds(WIDE * (2 * q + e), WIDE)]
 
     def single(c, q, b):
-        return g.at[c, pl.ds(4 * q + 2 * e + b, 1)]
+        return g.at[c, pl.ds(WIDE * (2 * q + e) + WIDE // 2 * b, WIDE // 2)]
 
     def first(q, w):
         dev = ident(at(pos1 + 1 + 2 * w, pos2), e, y)
@@ -379,12 +471,8 @@
         return remote(single(c, q, w), single(c, q, w), sd.at[q, o, w], rd.at[q, o, w], twin)
 
     def across(q, core):
-        part = g.at[:, pl.ds(4 * q + 2 * core, 2)]
+        part = g.at[:, pl.ds(WIDE * (2 * q + core), WIDE)]
         return remote(part, part, se.at[q], re.at[q], twin)
-
-    def out_copy(q):
-        part = (slice(None), pl.ds(4 * q, 4))
-        return pltpu.make_async_copy(g.at[part], out_ref.at[part], lsem.at[q])
 
     def wave0(q, carry):
         for w in range(2):
@@ -430,7 +518,6 @@
 
     def wave5(q, carry):
         across(q, 1 - e).wait_recv()
-        out_copy(q).start()
         return carry
 
     def off_in(d, carry):
@@ -489,7 +576,6 @@
                 third(q, o, w).wait_send()
                 fourth(q, o, w).wait_send()
         across(q, e).wait_send()
-        out_copy(q).wait()
         return carry
 
     lax.fori_loop(0, CHUNKS, drain_chunk, 0)
@@ -509,10 +595,9 @@
             jax.ShapeDtypeStruct(offs.shape, f32),
         ),
         in_specs=[pl.BlockSpec(memory_space=pltpu.SMEM), vm, vm],
-        out_specs=(pl.BlockSpec(memory_space=pl.ANY), vm),
+        out_specs=(vm, vm),
         scratch_shapes=[
             pltpu.VMEM((2, 16, slots, rows, width), bf16),
-            pltpu.VMEM((16, blocks, rows, width), bf16),
             pltpu.VMEM((16,) + offs.shape, f32),
             pltpu.VMEM((ny + 2,) + offs.shape, f32),
             dma((16,)), dma((16,)), dma((16,)), dma((16,)),
@@ -520,43 +605,73 @@
             dma((n, 4, 2)), dma((n, 4, 2)), dma((n, 4, 2)), dma((n, 4, 2)),
             dma((n,)), dma((n,)),
             dma((16,)), dma((16,)), dma((ny,)), dma((ny,)), dma, dma,
-            dma((n,)),
         ],
         compiler_params=pltpu.CompilerParams(
-            collective_id=0, has_side_effects=True, vmem_limit_bytes=32 << 20
+            collective_id=0, has_side_effects=True, vmem_limit_bytes=16 << 20
         ),
+        cost_estimate=pl.CostEstimate(flops=20 * 10**9, bytes_accessed=1 << 20, transcendentals=0),
         name="gather_factors",
     )(idx, packed, offs)
 
 
-def apply_kernel(p_ref, g_ref, u_ref):
-    count, _, rows, width = p_ref.shape
-    packed = p_ref[...].reshape(count * rows, width)
-    tiles = {ij: packed[t * GW : (t + 1) * GW] for t, ij in enumerate(TILES)}
-    lines = [
-        jnp.concatenate([tiles[i, j] if j >= i else tiles[j, i].T for j in range(4)], axis=1)
-        for i in range(4)
-    ]
-    u_ref[0] = jnp.dot(
-        g_ref[0], jnp.concatenate(lines, axis=0), preferred_element_type=f32
-    ).astype(bf16)
-
-
-def apply(packed, gradients):
+def apply_kernel(p_ref, o_ref, g_ref, u_any, tops_ref, u_ref, f_ref, out_sem):
+    blocks = g_ref.shape[0]
+    rows = p_ref.shape[2]
+
+    def save(k):
+        return pltpu.make_async_copy(u_ref.at[k], u_any.at[k], out_sem.at[k])
+
+    for i in range(MAXS):
+        tops_ref[i] = jnp.max(o_ref[i : i + 1, :])
+
+    def assemble(k, slot):
+        packed = p_ref[:, k].reshape(p_ref.shape[0] * rows, GW)
+        for t, (i, j) in enumerate(TILES):
+            tile = packed[grp(t)]
+            f_ref[slot, grp(i), grp(j)] = tile
+            if i != j:
+                f_ref[slot, grp(j), grp(i)] = tile.T
+
+    def turn(k, slot):
+        u_ref[k] = dot(g_ref[k], f_ref[slot]).astype(bf16)
+
+    assemble(0, 0)
+
+    def step(n, carry):
+        k = 2 * n
+        assemble(k + 1, 1)
+        turn(k, 0)
+        assemble(jnp.minimum(k + 2, blocks - 1), 0)
+        turn(k + 1, 1)
+        save(k).start()
+        save(k + 1).start()
+        return carry
+
+    lax.fori_loop(0, blocks // 2, step, 0)
+    for k in range(blocks):
+        save(k).wait()
+
+
+def apply(packed, tops, gradients):
     blocks, cols, size = gradients.shape
-    chips, _, rows, width = packed.shape
+    anywhere = pl.BlockSpec(memory_space=pl.ANY)
+    vm = pl.BlockSpec(memory_space=pltpu.VMEM)
     return pl.pallas_call(
         apply_kernel,
-        grid=(blocks,),
-        out_shape=jax.ShapeDtypeStruct((blocks, cols, size), bf16),
-        in_specs=[
-            pl.BlockSpec((chips, 1, rows, width), lambda k: (0, k, 0, 0)),
-            pl.BlockSpec((1, cols, size), lambda k: (k, 0, 0)),
+        out_shape=(
+            jax.ShapeDtypeStruct((blocks, cols, size), bf16),
+            jax.ShapeDtypeStruct((MAXS,), f32),
+        ),
+        in_specs=[vm, vm, vm],
+        out_specs=(anywhere, pl.BlockSpec(memory_space=pltpu.SMEM)),
+        scratch_shapes=[
+            pltpu.VMEM((blocks, cols, size), bf16),
+            pltpu.VMEM((2, size, size), bf16),
+            pltpu.SemaphoreType.DMA((blocks,)),
         ],
-        out_specs=pl.BlockSpec((1, cols, size), lambda k: (k, 0, 0)),
-        compiler_params=pltpu.CompilerParams(vmem_limit_bytes=32 << 20),
+        compiler_params=pltpu.CompilerParams(vmem_limit_bytes=28 << 20),
         name="apply_factors",
-    )(packed, gradients)
+    )(packed, tops, gradients)
 
 
 BLK = AXES[:3]
@@ -564,12 +679,16 @@
 
 def per_device(ny, statistics, gradients, live_counts, slot_row, sweeps):
     matrices = statistics[0]
+    live_counts, slot_row, sweeps, matrices = (
+        pltpu.with_memory_space_constraint(value, pltpu.HBM)
+        for value in (live_counts, slot_row, sweeps, matrices)
+    )
     packed, offs, where_of = jacobi(
-        live_counts[0], slot_row[0], sweeps[0], gradients.shape[1], matrices
+        live_counts, slot_row, sweeps, gradients.shape[1], matrices
     )
     pieces, tops = gather(where_of, packed, offs, ny)
-    updates = apply(pieces, jnp.swapaxes(gradients[0], 1, 2))
-    return jnp.swapaxes(updates, 1, 2)[None], tops[:MAXS, 0]
+    updates, off_max = apply(pieces, tops, jnp.swapaxes(gradients[0], 1, 2))
+    return jnp.swapaxes(updates, 1, 2)[None], off_max
 
 
 def solution(mesh):

time: 117 us -> 110 us (0.940)
  local copies, waits for them, and re-layouts: 7.26 us -> 0.02 us
    pallas_call x1, Pallas kernels: 20.1 us -> 43.3 us  [jacobi(): pl.pallas_call(jacobi_kernel, out_shape=(jax.ShapeDtypeStruct((slots, len...]
    pallas_call x1, Pallas kernels: 79.5 us -> 58.4 us  [gather(): pl.pallas_call(functools.partial(gather_kernel, ny), out_shape=(jax.Shape...]
    unnamed x10 -> x4, local copies, waits for them, and re-layouts: 6.63 us -> 0.02 us
    pallas_call x1, Pallas kernels: 10.3 us -> 7.11 us  [apply(): pl.pallas_call(apply_kernel, out_shape=(jax.ShapeDtypeStruct((blocks, col...]
where the time goes in v3:
time: 110 us
  Pallas kernels  109 us (99%)
    pallas_call x1, Pallas kernels, gather(): pl.pallas_call(functools.partial(gather_kernel, ny), out_shape=(jax.Shape...  58.4 us
    pallas_call x1, Pallas kernels, jacobi(): pl.pallas_call(jacobi_kernel, out_shape=(jax.ShapeDtypeStruct((slots, len...  43.3 us
    pallas_call x1, Pallas kernels, apply(): pl.pallas_call(apply_kernel, out_shape=(jax.ShapeDtypeStruct((blocks, col...  7.11 us

profile of v3, /device:TPU:1, one launch (start us, length us, event | category | flops | bytes accessed | tf_op | source)
XLA Modules:
  0.0 109.7 jit_solution(133327444878227306)
XLA Ops:
  0.6 0.0 slice-start
  0.6 43.3 %jacobi.1 = (bf16[2,1280,128]{2,1,0:T(8,128)(2,1)S(1)}, f32[8,128]{1,0:T(8,128)S(1)}, s32[16]{0:T(128)S(1)}) custom-call(s32[1,32]{1,0:T(1,128)} %live_any.1, s32[1,64]{1,0:T(1,128)} %row_any.1, s32[1,2]{1,0:T(1,128)} %sweeps_any.1, f32[2,512,512]{2,1,0:T(8,128)} %bitcast.11), custom_call_target="tpu_custom_call" | custom-call | flops 20000000000 | bytes 1048576 | tf_op jit(solution)/shard_map/jacobi/pallas_call | solution.py:302
  44.0 0.0 slice-start.1
  44.0 58.4 %gather_factors.1 = (bf16[16,16,80,128]{3,2,1,0:T(8,128)(2,1)S(1)}, f32[8,128]{1,0:T(8,128)S(1)}) custom-call(s32[16]{0:T(128)S(1)} %get-tuple-element.9.idx_ref, bf16[2,1280,128]{2,1,0:T(8,128)(2,1)S(1)} %get-tuple-element.10.f_ref, f32[8,128]{1,0:T(8,128)S(1)} %get-tuple-element.11.off_ref), custom_call_target="tpu_custom_call" | custom-call | flops 20000000000 | bytes 1048576 | tf_op jit(solution)/shard_map/gather_factors/pallas_call | solution.py:591
  102.4 0.0 slice-done
  102.4 0.0 slice-done.1
  102.5 7.1 %apply_factors.1 = (bf16[16,448,512]{2,1,0:T(8,128)(2,1)}, f32[2]{0:T(128)}) custom-call(bf16[16,16,80,128]{3,2,1,0:T(8,128)(2,1)S(1)} %get-tuple-element.12.p_ref, f32[8,128]{1,0:T(8,128)S(1)} %get-tuple-element.13.o_ref, bf16[16,448,512]{2,1,0:T(8,128)(2,1)S(1)} %bitcast.9), custom_call_target="tpu_custom_call" | custom-call | tf_op jit(solution)/shard_map/apply_factors/pallas_call | solution.py:659
  (1 shorter events, 0.0 us)
Async XLA Ops:
  0.6 101.8 %slice-start = ((s8[7340032]{0:T(1024)(128)(4,1)}), s8[4194304]{0:T(1024)(128)(4,1)S(1)}, s32[]{:S(2)}) async-start(s8[7340032]{0:T(1024)(128)(4,1)} %bitcast.7), calls=%async_computation | async-start | bytes 8388608
  44.0 58.4 %slice-start.1 = ((s8[7340032]{0:T(1024)(128)(4,1)}), s8[3145728]{0:T(1024)(128)(4,1)S(1)}, s32[]{:S(2)}) async-start(s8[7340032]{0:T(1024)(128)(4,1)} %bitcast.7), calls=%async_computation.1 | async-start | bytes 6291456

commit v4 on v3

--- a/solution.py
+++ b/solution.py
@@ -13,7 +13,7 @@
 pairings = ((0, 1, 2, 3), (0, 2, 1, 3), (0, 3, 1, 2))
 f32, bf16 = jnp.float32, jnp.bfloat16
 TOL = 1e-6
-EASY = 1.5
+EASY = 0.8
 TILES = [(i, j) for i in range(4) for j in range(i, 4)]
 
 
@@ -79,16 +79,10 @@
         w_ref[j] = alpha * w_ref[j]
 
 
-def sweep_body(slots, m_ref, v_ref, y_ref, w_ref, b_ref, p_ref, r_ref):
+def sweep_body(slots, m_ref, v_ref, w_ref, b_ref, p_ref):
     mask = eye_mask(GW)
     identity = mask.astype(f32)
     eye2 = two(identity, identity)
-
-    def rot(s, h):
-        return (
-            (r_ref[s, h, 0], r_ref[s, h, 1]),
-            (r_ref[s, h, 2], r_ref[s, h, 3]),
-        )
 
     def block(s, rows, cols):
         lines = [two(m_ref[s, grp(a), grp(cols[0])], m_ref[s, grp(a), grp(cols[1])]) for a in rows]
@@ -99,16 +93,16 @@
             for j, b in enumerate(cols):
                 m_ref[s, grp(a), grp(b)] = value[grp(i), grp(j)]
 
-    def settle(s, halves):
+    def settle(n, s, halves, turns, own):
         for h in range(2):
-            r, rt = rot(s, h)
-            store(s, halves[h], halves[h], dot3(rt, split(y_ref[s, h])))
+            r, rt = turns[n, h]
+            store(s, halves[h], halves[h], dot3(rt, split(own[n, h])))
             cols = two(v_ref[s, :, grp(halves[h][0])], v_ref[s, :, grp(halves[h][1])])
             turned = dot3(split(cols), r)
             for i in range(2):
                 v_ref[s, :, grp(halves[h][i])] = turned[:, grp(i)]
 
-    last, diagonals = None, {}
+    last, diagonals, turns, own = None, {}, {}, {}
     for pairing in pairings:
         halves = (pairing[:2], pairing[2:])
         peak = None
@@ -138,10 +132,7 @@
             cb = c.astype(bf16)
             p = dot(cb, apart(cb))
             t = eye2 + c
-            pb = p.astype(bf16)
-            stacked = dot(jnp.concatenate([t.astype(bf16), pb], axis=0), apart(pb))
-            t = t + stacked[:GW]
-            w = alpha * (t + dot(t.astype(bf16), apart(stacked[GW:].astype(bf16))))
+            w = alpha * (t + dot(t.astype(bf16), apart(p.astype(bf16))))
             done = two(*[
                 dot3_packed(split(mats[h]), split(w[:, grp(h)])) for h in range(2)
             ])
@@ -152,7 +143,7 @@
             kept[n] = ang
             peak = bound if peak is None else jnp.maximum(peak, bound)
             if last is not None:
-                settle(s, last)
+                settle(n, s, last, turns, own)
         peak = jnp.max(peak)
 
         @pl.when(peak > EASY)
@@ -167,18 +158,16 @@
                 q = identity - 0.5 * dot3_packed(sat, sx)
                 p = 2.0 * w - identity
                 sp, sq, sxt = split(p), split(q), split(x.T)
-                for i in range(2):
-                    r_ref[s, h, i] = jnp.concatenate([two(sp[i], sx[i]), two(-sxt[i], sq[i])], axis=0)
-                    r_ref[s, h, 2 + i] = jnp.concatenate(
-                        [two(sp[i], -sx[i]), two(sxt[i], sq[i])], axis=0
-                    )
+                turns[n, h] = (
+                    [jnp.concatenate([two(sp[i], sx[i]), two(-sxt[i], sq[i])], axis=0) for i in range(2)],
+                    [jnp.concatenate([two(sp[i], -sx[i]), two(sxt[i], sq[i])], axis=0) for i in range(2)],
+                )
         for n, s in enumerate(slots):
-            r0, rt0 = rot(s, 0)
-            r1, _ = rot(s, 1)
+            (r0, rt0), (r1, _) = turns[n, 0], turns[n, 1]
             z = dot3(rt0, split(dot3(split(block(s, halves[0], halves[1])), r1)))
             for h, r in enumerate((r0, r1)):
                 y = dot3(split(block(s, halves[h], halves[h])), r)
-                y_ref[s, h] = y
+                own[n, h] = y
                 full = r[0].astype(f32) + r[1].astype(f32)
                 row = jnp.sum(full * y, axis=0, keepdims=True)
                 for i in range(2):
@@ -186,8 +175,8 @@
             store(s, halves[0], halves[1], z)
             store(s, halves[1], halves[0], z.T)
         last = halves
-    for s in slots:
-        settle(s, last)
+    for n, s in enumerate(slots):
+        settle(n, s, last, turns, own)
 
 
 def off_norm(matrix, mask):
@@ -219,7 +208,7 @@
 
 def jacobi_kernel(
     live_any, row_any, sweeps_any, stats_ref,
-    f_ref, off_ref, place_ref, m_ref, v_ref, y_ref, w_ref, b_ref, p_ref, r_ref, live_s, row_s, sweeps_s, sem,
+    f_ref, off_ref, place_ref, m_ref, v_ref, w_ref, b_ref, p_ref, live_s, row_s, sweeps_s, sem,
 ):
     small = [
         pltpu.make_async_copy(src, dst, sem.at[2 + i])
@@ -227,8 +216,13 @@
             ((live_any, live_s), (row_any, row_s), (sweeps_any, sweeps_s))
         )
     ]
+    def load(s):
+        return pltpu.make_async_copy(stats_ref.at[s], m_ref.at[s], sem.at[s])
+
     for copy in small:
         copy.start()
+    for s in range(2):
+        load(s).start()
     for copy in small:
         copy.wait()
     live_ref, row_ref, sweeps_ref = live_s.at[0], row_s.at[0], sweeps_s.at[0]
@@ -240,32 +234,26 @@
     n0 = jnp.where(own > 0, sweeps_ref[0], 0)
     n1 = jnp.where(own > 1, sweeps_ref[1], 0)
 
-    def load(s):
-        return pltpu.make_async_copy(stats_ref.at[s], m_ref.at[s], sem.at[s])
-
-    for s, n in enumerate((n0, n1)):
-        pl.when(n > 0)(lambda s=s: load(s).start())
-
-    for k in range(place_ref.shape[0]):
-        place_ref[k] = 0
-
-    def note_place(j, carry):
-        @pl.when(lax.rem(j, 2) < live_ref[j // 2])
-        def _():
-            place_ref[row_ref[j]] = lax.rem(j // 2, 2) * devices + (j // 4) * 2 + lax.rem(j, 2)
-
-        return carry
-
-    lax.fori_loop(0, 2 * devices, note_place, 0)
+    spare = place_ref.shape[0] - 1
+
+    def note_place(d, carry):
+        base = lax.rem(d, 2) * devices + (d // 2) * 2
+        for i in range(2):
+            place_ref[jnp.where(i < live_ref[d], row_ref[2 * d + i], spare)] = base + i
+        return carry
+
+    lax.fori_loop(0, devices, note_place, 0, unroll=4)
     off_ref[...] = jnp.zeros_like(off_ref)
-    scratch = (m_ref, v_ref, y_ref, w_ref, b_ref, p_ref, r_ref)
+    scratch = (m_ref, v_ref, w_ref, b_ref, p_ref)
 
     for s, n in enumerate((n0, n1)):
 
         @pl.when(n > 0)
         def _(s=s):
             v_ref[s] = mask.astype(f32)
-            load(s).wait()
+
+    for s in range(2):
+        load(s).wait()
 
     def sweep(i, carry):
         a0, a1 = n0 > i, n1 > i
@@ -304,18 +292,16 @@
         out_shape=(
             jax.ShapeDtypeStruct((slots, len(TILES) * GW, GW), bf16),
             jax.ShapeDtypeStruct((8, GW), f32),
-            jax.ShapeDtypeStruct((blocks,), jnp.int32),
+            jax.ShapeDtypeStruct((blocks + 8,), jnp.int32),
         ),
         in_specs=[pl.BlockSpec(memory_space=pltpu.HBM)] * 4,
         out_specs=(vm, vm, sm),
         scratch_shapes=[
             pltpu.VMEM((slots, size, size), f32),
             pltpu.VMEM((slots, size, size), f32),
-            pltpu.VMEM((slots, 2, 2 * GW, 2 * GW), f32),
             pltpu.VMEM((2 * slots, GW, GW), f32),
             pltpu.VMEM((2 * slots, GW, GW), f32),
             pltpu.VMEM((2 * slots, GW, GW), f32),
-            pltpu.VMEM((slots, 2, 4, 2 * GW, 2 * GW), bf16),
             pltpu.SMEM(live.shape, jnp.int32),
             pltpu.SMEM(slot_row.shape, jnp.int32),
             pltpu.SMEM(sweeps.shape, jnp.int32),
@@ -333,6 +319,12 @@
 MESH_ID = pl.DeviceIdType.MESH
 
 
+STEPS = sorted(
+    ((a, b) for a in range(4) for b in range(4) if a or b),
+    key=lambda ab: -(min(ab[0], 4 - ab[0]) + min(ab[1], 4 - ab[1])),
+)
+
+
 def gather_kernel(ny, idx_ref, f_ref, off_ref, g, omax_ref,
                   spread, offs, ostage,
                   s1, r1, s2, r2, sa, ra, sb, rb, sc, rc, sd, rd, se, re,
@@ -352,19 +344,24 @@
 
     twin = ident(chip, 1 - e, y)
 
+    def ahead(d):
+        a, b = STEPS[d - 1]
+        return lax.rem(x + a, 4) * 4 + lax.rem(z + b, 4)
+
+    def behind(d):
+        a, b = STEPS[d - 1]
+        return lax.rem(x + 4 - a, 4) * 4 + lax.rem(z + 4 - b, 4)
+
     def peer(d):
-        return ident(lax.rem(chip + d, 16), e, y)
+        return ident(ahead(d), e, y)
 
     def level(d):
         return ident(chip, e, lax.rem(y + d, ny))
 
     barrier = pltpu.get_barrier_semaphore()
 
-    def greet(d, carry):
+    for d in range(1, 16):
         pl.semaphore_signal(barrier, inc=1, device_id=peer(d), device_id_type=MESH_ID)
-        return carry
-
-    lax.fori_loop(1, 16, greet, 0)
     for d in range(1, ny):
         pl.semaphore_signal(barrier, inc=1, device_id=level(d), device_id_type=MESH_ID)
     pl.semaphore_signal(barrier, inc=1, device_id=twin, device_id_type=MESH_ID)
@@ -374,11 +371,10 @@
         return f_ref.at[:, pl.ds(pl.multiple_of(c * rows, 16), rows), :]
 
     def spread_copy(d):
-        target = lax.rem(chip + d, 16)
-        return remote(my_rows(target), spread.at[e, chip], s1.at[d], r1.at[d], peer(d))
+        return remote(my_rows(ahead(d)), spread.at[e, chip], s1.at[d], r1.at[d], peer(d))
 
     def pass_copy(d):
-        source = lax.rem(chip + 16 - d, 16)
+        source = behind(d)
         return remote(spread.at[e, source], spread.at[e, source], s2.at[d], r2.at[d], twin)
 
     def own_copy():
@@ -387,34 +383,19 @@
     def off_copy(d):
         return remote(off_ref, offs.at[d], so.at[d], ro.at[d], peer(d))
 
-    def go(copy):
-        def step(d, carry):
-            copy(d).start()
-            return carry
-        return step
-
-    lax.fori_loop(1, 16, go(spread_copy), 0)
-    lax.fori_loop(1, 16, go(off_copy), 0)
+    for d in range(1, 16):
+        spread_copy(d).start()
     own_copy().start()
     spread[e, chip] = f_ref[:, pl.ds(pl.multiple_of(chip * rows, 16), rows), :]
     offs[0] = off_ref[...]
-
-    def relay_twin(d, carry):
-        source = lax.rem(chip + 16 - d, 16)
-        remote(my_rows(chip), spread.at[e, source], s1.at[d], r1.at[d], peer(d)).wait_recv()
+    for d in range(1, 16):
+        spread_copy(d).wait_recv()
         pass_copy(d).start()
-        return carry
-
-    lax.fori_loop(1, 16, relay_twin, 0)
-
-    def twin_in(d, carry):
-        source = lax.rem(chip + 16 - d, 16)
+    for d in range(16):
+        source = behind(d) if d else chip
         remote(
             spread.at[1 - e, source], spread.at[1 - e, source], s2.at[d], r2.at[d], twin
         ).wait_recv()
-        return carry
-
-    lax.fori_loop(0, 16, twin_in, 0)
 
     for q in range(CHUNKS):
         for b in range(WIDE):
@@ -520,50 +501,42 @@
         across(q, 1 - e).wait_recv()
         return carry
 
-    def off_in(d, carry):
-        remote(off_ref, offs.at[d], so.at[d], ro.at[d], peer(d)).wait_recv()
-        return carry
-
-    lax.fori_loop(1, 16, off_in, 0)
+    def level_copy(d):
+        return remote(ostage.at[0], ostage.at[d], sp.at[d], rp.at[d], level(d))
+
+    def core_copy():
+        return remote(ostage.at[ny], ostage.at[ny + 1], sq, rq, twin)
+
+    lax.fori_loop(0, CHUNKS, wave0, 0)
+    for d in range(1, 16):
+        off_copy(d).start()
+    lax.fori_loop(0, CHUNKS, wave1, 0)
     top = offs[0]
     for d in range(1, 16):
+        off_copy(d).wait_recv()
         top = jnp.maximum(top, offs[d])
     ostage[0] = top
-
-    def level_copy(d):
-        return remote(ostage.at[0], ostage.at[d], sp.at[d], rp.at[d], level(d))
-
-    lax.fori_loop(0, CHUNKS, wave0, 0)
+    lax.fori_loop(0, CHUNKS, wave2, 0)
     for d in range(1, ny):
         level_copy(d).start()
-
-    lax.fori_loop(0, CHUNKS, wave1, 0)
-
+    lax.fori_loop(0, CHUNKS, wave3, 0)
     for d in range(1, ny):
         level_copy(d).wait_recv()
         top = jnp.maximum(top, ostage[d])
     ostage[ny] = top
-
-    def core_copy():
-        return remote(ostage.at[ny], ostage.at[ny + 1], sq, rq, twin)
-
-    lax.fori_loop(0, CHUNKS, wave2, 0)
+    lax.fori_loop(0, CHUNKS - 1, wave4, 0)
     core_copy().start()
-    lax.fori_loop(0, CHUNKS, wave3, 0)
+    wave4(CHUNKS - 1, 0)
+    lax.fori_loop(0, CHUNKS, wave5, 0)
     core_copy().wait_recv()
     omax_ref[...] = jnp.maximum(top, ostage[ny + 1])
-    lax.fori_loop(0, CHUNKS, wave4, 0)
-    lax.fori_loop(0, CHUNKS, wave5, 0)
 
     own_copy().wait_send()
 
-    def drain(d, carry):
+    for d in range(1, 16):
         spread_copy(d).wait_send()
         pass_copy(d).wait_send()
         off_copy(d).wait_send()
-        return carry
-
-    lax.fori_loop(1, 16, drain, 0)
     for d in range(1, ny):
         level_copy(d).wait_send()
     core_copy().wait_send()
@@ -581,10 +554,9 @@
     lax.fori_loop(0, CHUNKS, drain_chunk, 0)
 
 
-def gather(idx, packed, offs, ny):
+def gather(idx, blocks, packed, offs, ny):
     slots, length, width = packed.shape
     rows = length // 16
-    blocks = idx.shape[0]
     vm = pl.BlockSpec(memory_space=pltpu.VMEM)
     dma = pltpu.SemaphoreType.DMA
     n = CHUNKS
@@ -686,7 +658,7 @@
     packed, offs, where_of = jacobi(
         live_counts, slot_row, sweeps, gradients.shape[1], matrices
     )
-    pieces, tops = gather(where_of, packed, offs, ny)
+    pieces, tops = gather(where_of, gradients.shape[1], packed, offs, ny)
     updates, off_max = apply(pieces, tops, jnp.swapaxes(gradients[0], 1, 2))
     return jnp.swapaxes(updates, 1, 2)[None], off_max
 

time: 110 us -> 106 us (0.964); the launches traced: 110 us -> 107 us
  Pallas kernels: 109 us -> 106 us
    pallas_call x1, Pallas kernels: 58.4 us -> 48.5 us  [gather(): pl.pallas_call(functools.partial(gather_kernel, ny), out_shape=(jax.Shape...]
    pallas_call x1, Pallas kernels: 43.3 us -> 50.3 us  [jacobi(): pl.pallas_call(jacobi_kernel, out_shape=(jax.ShapeDtypeStruct((slots, len...]
where the time goes in v4:
time: 106 us; the launch traced here: 107 us
  Pallas kernels  106 us (100%)
    pallas_call x1, Pallas kernels, jacobi(): pl.pallas_call(jacobi_kernel, out_shape=(jax.ShapeDtypeStruct((slots, len...  50.3 us
    pallas_call x1, Pallas kernels, gather(): pl.pallas_call(functools.partial(gather_kernel, ny), out_shape=(jax.Shape...  48.5 us
    pallas_call x1, Pallas kernels, apply(): pl.pallas_call(apply_kernel, out_shape=(jax.ShapeDtypeStruct((blocks, col...  7.11 us

profile of v4, /device:TPU:1, one launch (start us, length us, event | category | flops | bytes accessed | tf_op | source)
XLA Modules:
  0.0 106.8 jit_solution(14873528571464548430)
XLA Ops:
  0.6 0.0 slice-start
  0.6 50.3 %jacobi.1 = (bf16[2,1280,128]{2,1,0:T(8,128)(2,1)S(1)}, f32[8,128]{1,0:T(8,128)S(1)}, s32[24]{0:T(128)S(1)}) custom-call(s32[1,32]{1,0:T(1,128)} %live_any.1, s32[1,64]{1,0:T(1,128)} %row_any.1, s32[1,2]{1,0:T(1,128)} %sweeps_any.1, f32[2,512,512]{2,1,0:T(8,128)} %bitcast.11), custom_call_target="tpu_custom_call" | custom-call | flops 20000000000 | bytes 1048576 | tf_op jit(solution)/shard_map/jacobi/pallas_call | solution.py:290
  51.0 0.0 slice-start.1
  51.0 48.5 %gather_factors.1 = (bf16[16,16,80,128]{3,2,1,0:T(8,128)(2,1)S(1)}, f32[8,128]{1,0:T(8,128)S(1)}) custom-call(s32[24]{0:T(128)S(1)} %get-tuple-element.9.idx_ref, bf16[2,1280,128]{2,1,0:T(8,128)(2,1)S(1)} %get-tuple-element.10.f_ref, f32[8,128]{1,0:T(8,128)S(1)} %get-tuple-element.11.off_ref), custom_call_target="tpu_custom_call" | custom-call | flops 20000000000 | bytes 1048576 | tf_op jit(solution)/shard_map/gather_factors/pallas_call | solution.py:563
  99.6 0.0 slice-done
  99.6 0.0 slice-done.1
  99.6 7.1 %apply_factors.1 = (bf16[16,448,512]{2,1,0:T(8,128)(2,1)}, f32[2]{0:T(128)}) custom-call(bf16[16,16,80,128]{3,2,1,0:T(8,128)(2,1)S(1)} %get-tuple-element.12.p_ref, f32[8,128]{1,0:T(8,128)S(1)} %get-tuple-element.13.o_ref, bf16[16,448,512]{2,1,0:T(8,128)(2,1)S(1)} %bitcast.9), custom_call_target="tpu_custom_call" | custom-call | tf_op jit(solution)/shard_map/apply_factors/pallas_call | solution.py:631
  (1 shorter events, 0.0 us)
Async XLA Ops:
  0.6 98.9 %slice-start = ((s8[7340032]{0:T(1024)(128)(4,1)}), s8[4194304]{0:T(1024)(128)(4,1)S(1)}, s32[]{:S(2)}) async-start(s8[7340032]{0:T(1024)(128)(4,1)} %bitcast.7), calls=%async_computation | async-start | bytes 8388608
  51.0 48.6 %slice-start.1 = ((s8[7340032]{0:T(1024)(128)(4,1)}), s8[3145728]{0:T(1024)(128)(4,1)S(1)}, s32[]{:S(2)}) async-start(s8[7340032]{0:T(1024)(128)(4,1)} %bitcast.7), calls=%async_computation.1 | async-start | bytes 6291456

commit v5 on v4

--- a/solution.py
+++ b/solution.py
@@ -274,13 +274,13 @@
 
     lax.fori_loop(0, MAXS, sweep, 0)
 
-    @pl.when(n0 > 0)
+    @pl.when((n0 > 0) & (n1 == 0))
     def _():
         finish((0,), m_ref, v_ref, f_ref, mask)
 
     @pl.when(n1 > 0)
     def _():
-        finish((1,), m_ref, v_ref, f_ref, mask)
+        finish((0, 1), m_ref, v_ref, f_ref, mask)
 
 
 def jacobi(live, slot_row, sweeps, blocks, stats):

time: 106 us -> 107 us (level)
    pallas_call x1, Pallas kernels: 48.5 us -> 96.7 us  [gather(): pl.pallas_call(functools.partial(gather_kernel, ny), out_shape=(jax.Shape...]
    pallas_call x1, Pallas kernels: 50.3 us -> 2.33 us  [jacobi(): pl.pallas_call(jacobi_kernel, out_shape=(jax.ShapeDtypeStruct((slots, len...]
where the time goes in v5:
time: 107 us
  Pallas kernels  106 us (99%)
    pallas_call x1, Pallas kernels, gather(): pl.pallas_call(functools.partial(gather_kernel, ny), out_shape=(jax.Shape...  96.7 us
    pallas_call x1, Pallas kernels, apply(): pl.pallas_call(apply_kernel, out_shape=(jax.ShapeDtypeStruct((blocks, col...  7.1 us
    pallas_call x1, Pallas kernels, jacobi(): pl.pallas_call(jacobi_kernel, out_shape=(jax.ShapeDtypeStruct((slots, len...  2.33 us

profile of v5, /device:TPU:1, one launch (start us, length us, event | category | flops | bytes accessed | tf_op | source)
XLA Modules:
  0.0 107.0 jit_solution(1232525966181651666)
XLA Ops:
  0.6 0.0 slice-start
  0.6 2.3 %jacobi.1 = (bf16[2,1280,128]{2,1,0:T(8,128)(2,1)S(1)}, f32[8,128]{1,0:T(8,128)S(1)}, s32[24]{0:T(128)S(1)}) custom-call(s32[1,32]{1,0:T(1,128)} %live_any.1, s32[1,64]{1,0:T(1,128)} %row_any.1, s32[1,2]{1,0:T(1,128)} %sweeps_any.1, f32[2,512,512]{2,1,0:T(8,128)} %bitcast.11), custom_call_target="tpu_custom_call" | custom-call | flops 20000000000 | bytes 1048576 | tf_op jit(solution)/shard_map/jacobi/pallas_call | solution.py:290
  3.0 0.0 slice-start.1
  3.0 96.7 %gather_factors.1 = (bf16[16,16,80,128]{3,2,1,0:T(8,128)(2,1)S(1)}, f32[8,128]{1,0:T(8,128)S(1)}) custom-call(s32[24]{0:T(128)S(1)} %get-tuple-element.9.idx_ref, bf16[2,1280,128]{2,1,0:T(8,128)(2,1)S(1)} %get-tuple-element.10.f_ref, f32[8,128]{1,0:T(8,128)S(1)} %get-tuple-element.11.off_ref), custom_call_target="tpu_custom_call" | custom-call | flops 20000000000 | bytes 1048576 | tf_op jit(solution)/shard_map/gather_factors/pallas_call | solution.py:563
  99.7 0.0 slice-done
  99.7 0.0 slice-done.1
  99.7 7.1 %apply_factors.1 = (bf16[16,448,512]{2,1,0:T(8,128)(2,1)}, f32[2]{0:T(128)}) custom-call(bf16[16,16,80,128]{3,2,1,0:T(8,128)(2,1)S(1)} %get-tuple-element.12.p_ref, f32[8,128]{1,0:T(8,128)S(1)} %get-tuple-element.13.o_ref, bf16[16,448,512]{2,1,0:T(8,128)(2,1)S(1)} %bitcast.9), custom_call_target="tpu_custom_call" | custom-call | tf_op jit(solution)/shard_map/apply_factors/pallas_call | solution.py:631
  (1 shorter events, 0.0 us)
Async XLA Ops:
  0.6 99.1 %slice-start = ((s8[7340032]{0:T(1024)(128)(4,1)}), s8[4194304]{0:T(1024)(128)(4,1)S(1)}, s32[]{:S(2)}) async-start(s8[7340032]{0:T(1024)(128)(4,1)} %bitcast.7), calls=%async_computation | async-start | bytes 8388608
  3.0 96.7 %slice-start.1 = ((s8[7340032]{0:T(1024)(128)(4,1)}), s8[3145728]{0:T(1024)(128)(4,1)S(1)}, s32[]{:S(2)}) async-start(s8[7340032]{0:T(1024)(128)(4,1)} %bitcast.7), calls=%async_computation.1 | async-start | bytes 6291456
